TPU v7x, 128 devices: a whole 4x4x4 slice. The times are simulated.
128 devices in a mesh: node: 16 (over y, x), grp: 8 (over z, core).
Axes of the slice: x: 4, y: 4, z: 4, core: 2. Of those that a mesh axis runs over, the one named last changes fastest.
Arguments:
- tokens: bfloat16 [49152, 1792], P(('node', 'grp')), may hold values from -6 to 6
- cotangent: bfloat16 [49152, 1792], P(('node', 'grp')), may hold values from -6 to 6
- gate_weight: bfloat16 [1792, 1024], P('node'), may hold values from -0.125 to 0.125
- up_weight: bfloat16 [1792, 1024], P('node'), may hold values from -0.125 to 0.125
- down_weight_t: bfloat16 [1792, 1024], P('node'), may hold values from -0.125 to 0.125
- error_memory: bfloat16 [8, 1792, 3072], P('grp', 'node'), may hold values from -4 to 4
- q_init: float32 [3, 1024, 32], replicated, may hold values from -6 to 6
Outputs:
- token_grad: bfloat16 [49152, 1792], P(('node', 'grp'))
- new_error: bfloat16 [8, 1792, 3072], P('grp', 'node')
- p_hat: float32 [3, 1792, 32], P(None, 'node')
- q_new: float32 [3, 1024, 32], replicated
All inputs are finite; a program needn't handle non-finite values.
Results may differ from a plain program's by a relative error of at most 0.012.
Values may be sent and summed in bfloat16 or wider, within the bound.
No kernel may reach another device: no remote copies, remote signals or barrier semaphores. Data moves between devices by JAX's collectives and lax.ppermute only.
A program may use at most 192 MiB of HBM per device.

v0:
```python
import functools
import math

import jax
import jax.numpy as jnp
from jax import lax
from jax.experimental import pallas as pl
from jax.experimental.pallas import tpu as pltpu
from jax.sharding import Mesh
from jax.sharding import PartitionSpec as P

Y, X, Z, C = "node_0", "node_1", "grp_0", "grp_1"
NODE = (Y, X)
GRP = (Z, C)
NODE_GRP = (Y, X, Z, C)
BF = jnp.bfloat16
F32 = jnp.float32
HIGH = lax.Precision.HIGHEST


def neighbour(value, stage, by):
    pairs = []
    for device in range(128):
        y, x, z, c = device // 32, device // 8 % 4, device // 2 % 4, device % 2
        if (c == 0) == (stage == 0):
            to = (y, (x + by) % 4, z, c)
        else:
            to = ((y + by) % 4, x, z, c)
        pairs.append((device, to[0] * 32 + to[1] * 8 + to[2] * 2 + to[3]))
    return lax.ppermute(value, NODE_GRP, pairs)


def other_core(value):
    return lax.ppermute(value, C, [(0, 1), (1, 0)])


def exchange(tiles, axis):
    return lax.all_to_all(tiles, axis, split_axis=0, concat_axis=0, tiled=True)


def dot(a, b, ca=1, cb=0, precision=None):
    return lax.dot_general(
        a, b, (((ca,), (cb,)), ((), ())), precision=precision, preferred_element_type=F32
    )


def call(body, out, grid=None, ins=None, outs=None, flops=0, scratch=(), vmem=24):
    params = {}
    if grid is not None:
        params.update(grid=grid, in_specs=ins, out_specs=outs)
    elif ins is not None:
        params.update(in_specs=ins)
    if flops:
        params["cost_estimate"] = pl.CostEstimate(
            flops=flops, bytes_accessed=1 << 20, transcendentals=0
        )
    return pl.pallas_call(
        body,
        out_shape=out,
        scratch_shapes=scratch,
        compiler_params=pltpu.CompilerParams(vmem_limit_bytes=(vmem + vmem // 2 + 6) << 20),
        **params,
    )


SCALAR = pl.BlockSpec(memory_space=pltpu.SMEM)
WHOLE = pl.BlockSpec(memory_space=pltpu.VMEM)


def struct(shape, kind=BF):
    return jax.ShapeDtypeStruct(shape, kind)


def near_struct(shape, kind=BF):
    return pltpu.VMEM(shape, kind)


def far_struct(shape, kind=BF):
    return pltpu.HBM(shape, kind)


def far(*values):
    return tuple(pltpu.with_memory_space_constraint(v, pltpu.HBM) for v in values)


def near(*values):
    return tuple(pltpu.with_memory_space_constraint(v, pltpu.VMEM) for v in values)


def gelu_parts(value):
    coeff = math.sqrt(2.0 / math.pi)
    inner = coeff * (value + 0.044715 * value * value * value)
    tanh_value = jnp.tanh(inner)
    activation = 0.5 * value * (1.0 + tanh_value)
    slope = 0.5 * (1.0 + tanh_value) + 0.5 * value * (1.0 - tanh_value * tanh_value) * coeff * (
        1.0 + 3.0 * 0.044715 * value * value
    )
    return (activation, slope)


def start_body(place_ref, gate_ref, up_ref, down_ref, own_ref):
    half = gate_ref.shape[1] // 2
    core = place_ref[16]
    for m, ref in enumerate((gate_ref, up_ref, down_ref)):
        own_ref[:, m * half : (m + 1) * half] = ref[:, pl.ds(pl.multiple_of(core * half, 128), half)]


def error_body(place_ref, e_ref, mine_ref, send_ref):
    half = mine_ref.shape[1] // 3
    units = 2 * half
    core = place_ref[16]
    for m in range(3):
        at = m * units + core * half
        mine_ref[:, m * half : (m + 1) * half] = e_ref[:, pl.ds(pl.multiple_of(at, 128), half)]
        at = m * units + (1 - core) * half
        send_ref[:, m * half : (m + 1) * half] = e_ref[:, pl.ds(pl.multiple_of(at, 128), half)]


def low_body(own_ref, left_ref, right_ref, low_ref, far_low_ref, far_high_ref):
    rows, at = own_ref.shape[0], far_low_ref.shape[0]
    low_ref[:rows] = own_ref[...]
    low_ref[rows:] = right_ref[...]
    far_low_ref[...] = left_ref[:at]
    far_high_ref[...] = right_ref[at:]


def high_body(far_low_ref, far_high_ref, left_ref, high_ref):
    at, rows = far_low_ref.shape[0], left_ref.shape[0]
    high_ref[:at] = far_low_ref[...]
    high_ref[at:rows] = far_high_ref[...]
    high_ref[rows:] = left_ref[...]


def picked(place_ref, width, rows):
    here = lax.broadcasted_iota(jnp.int32, (width, rows), 0) - place_ref[17]
    return jnp.where(here == lax.broadcasted_iota(jnp.int32, (width, rows), 1), 1.0, 0.0).astype(BF)


def roll_body(order_ref, own_ref, other_ref, out_ref, both_ref, scratch):
    tok, rows = own_ref.shape[0], out_ref.shape[1]
    both_ref[:tok] = own_ref[...]
    both_ref[tok:] = other_ref[...]
    scratch[:, :tok] = own_ref[...].T
    scratch[:, tok:] = other_ref[...].T
    for s in range(out_ref.shape[0]):
        out_ref[s] = scratch[pl.ds(pl.multiple_of(order_ref[s] * rows, 16), rows), :]


def rolled(order, own, other, rows):
    tok, width = own.shape
    roll, both = call(
        roll_body,
        (near_struct((width // rows, rows, 2 * tok)), near_struct((2 * tok, width))),
        ins=[SCALAR, WHOLE, WHOLE],
        scratch=[pltpu.VMEM((width, 2 * tok), BF)],
        vmem=5,
    )(order, own, other)
    return roll, both


def pair(ref, a, b, tok):
    at = pl.multiple_of(pl.program_id(0) * tok, 128)
    value = ref[4 * a + 2 * b : 4 * a + 2 * b + 2, :, pl.ds(at, tok)]
    return value.reshape(-1, tok)


def line(ref, b, tok):
    at = pl.multiple_of(pl.program_id(0) * tok, 128)
    return jnp.concatenate([ref[4 * a + b, :, pl.ds(at, tok)] for a in range(4)], axis=0)


def joined(ref):
    return ref[...].reshape(-1, ref.shape[-1])


def tokens_of(ref, tok):
    return ref.at[pl.ds(pl.multiple_of(pl.program_id(0) * tok, 128), tok), :]


def ahead_body(slots, t_ref, c_ref, *refs):
    tok = t_ref.shape[2] // 2
    out_ref = tokens_of(refs[-1], tok)
    units = out_ref.shape[-1] // 3
    gate_up, back = 0.0, 0.0
    if len(refs) > len(slots) + 1:
        part = tokens_of(refs[-2], tok)
        gate_up, back = part[:, : 2 * units], part[:, 2 * units :]
    for (a, b), piece in zip(slots, refs):
        gate_up = gate_up + dot(pair(t_ref, a, b, tok), piece[:, : 2 * units], 0, 0)
        back = back + dot(pair(c_ref, a, b, tok), piece[:, 2 * units :], 0, 0)
    out_ref[:, : 2 * units] = gate_up
    out_ref[:, 2 * units :] = back


def ahead(slots, t_roll, c_roll, pieces, partial=None):
    both, wide = t_roll.shape[2], pieces[0].shape[1]
    more = () if partial is None else near(partial)
    return call(
        functools.partial(ahead_body, slots),
        near_struct((both, wide), F32),
        grid=(2,),
        ins=[WHOLE] * (2 + len(pieces) + len(more)),
        outs=WHOLE,
        flops=2 * both * wide * pieces[0].shape[0] * len(pieces),
        vmem=5,
    )(*near(t_roll, c_roll), *pieces, *more)


def weight_part(t, c, grads):
    units = grads.shape[1] // 3
    return jnp.concatenate([dot(t, grads[:, : 2 * units]), dot(c, grads[:, 2 * units :])], axis=1)


def late_body(
    scale, groups, place_ref, part_all, t_ref, c_ref, low, high, q_ref, t_both, c_both,
    e_ref, e_other_ref, grads_ref, far_own, far_other, power_ref, total
):
    tok = t_ref.shape[2] // 2
    part_ref = tokens_of(part_all, tok)
    units = grads_ref.shape[-1] // 3
    gate_up, back = part_ref[:, : 2 * units], part_ref[:, 2 * units :]
    for b, piece in enumerate((low, high)):
        gate_up = gate_up + dot(pair(t_ref, 2, b, tok), piece[:, : 2 * units], 0, 0)
        back = back + dot(pair(c_ref, 2, b, tok), piece[:, 2 * units :], 0, 0)
    up_pre = gate_up[:, units:]
    activation, slope = gelu_parts(gate_up[:, :units])
    parts = (back * up_pre * slope, back * activation, activation * up_pre)
    parts = [part.astype(BF) for part in parts]
    for m, part in enumerate(parts):
        grads_ref[:, m * units : (m + 1) * units] = part
    far = weight_part(line(t_ref, 2, tok), line(c_ref, 2, tok), grads_ref).astype(BF)
    first = jnp.concatenate([dot(q_ref[m], parts[m], 1, 1) for m in range(2)], axis=0).astype(BF)
    second = dot(q_ref[2], parts[2], 1, 1).astype(BF)
    split = first.shape[0]
    top, bottom = dot(first, tokens_of(t_both, tok)[...]), dot(second, tokens_of(c_both, tok)[...])

    def start():
        far_own[...] = far
        total[:split], total[split:] = top, bottom

    def finish():
        far_other[...] = far
        value = jnp.concatenate([top + total[:split], bottom + total[split:]], axis=0)
        width, rows = value.shape[1], e_ref.shape[0]
        error = e_ref[...].astype(F32) + e_other_ref[...].astype(F32)
        error = jnp.concatenate(
            [dot(q_ref[m].astype(F32), error[:, m * units : (m + 1) * units], 1, 1) for m in range(3)],
            axis=0,
        )
        error_high = error.astype(BF)
        error_low = (error - error_high.astype(F32)).astype(BF)
        pick = picked(place_ref, width, rows)
        placed = dot(error_high, pick, 1, 1) + dot(error_low, pick, 1, 1)
        value = (value * scale + placed) * (1.0 / groups)
        step = value.shape[0] // groups
        for i in range(groups):
            power_ref[i] = value[i * step : (i + 1) * step].astype(BF)

    pl.when(pl.program_id(0) == 0)(start)
    pl.when(pl.program_id(0) == 1)(finish)


def near_body(t_one, c_one, t_three, c_three, grads_ref, *outs):
    one = weight_part(joined(t_one), joined(c_one), grads_ref).astype(BF)
    three = weight_part(joined(t_three), joined(c_three), grads_ref).astype(BF)
    for k in range(2):

        def put(k=k):
            outs[k][...] = one
            outs[2 + k][...] = three

        pl.when(pl.program_id(0) == k)(put)


def home_body(t_ref, c_ref, grads_ref, right_own, right_other, left_own, left_other, *outs):
    value = weight_part(joined(t_ref), joined(c_ref), grads_ref)
    rows = outs[0].shape[0]

    def put(k, a, b):
        total = (value + a[...].astype(F32) + b[...].astype(F32)).astype(BF)
        for i in range(4):
            outs[4 * k + i][...] = total[i * rows : (i + 1) * rows]

    pl.when(pl.program_id(0) == 0)(lambda: put(0, right_own, left_own))
    pl.when(pl.program_id(0) == 1)(lambda: put(1, right_other, left_other))


def spread_body(in_ref, out_ref):
    total = in_ref[0].astype(F32)
    for i in range(1, in_ref.shape[0]):
        total = total + in_ref[i].astype(F32)
    total = total.astype(BF)
    for i in range(out_ref.shape[0]):
        out_ref[i] = total


def spread(tiles, count):
    return call(spread_body, far_struct((count, *tiles.shape[1:])), vmem=4)(tiles)


def stacked(p_ref):
    return jnp.concatenate([p_ref[i].astype(F32) for i in range(p_ref.shape[0])], axis=0)


def right_body(
    scale, groups, place_ref, p_ref, t_ref, c_ref, y_ref, e_ref, e_other_ref, out_ref, total
):
    power = stacked(p_ref).astype(BF)
    rank = power.shape[0] // 3
    units = y_ref.shape[1] // 3
    seen = dot(power[: 2 * rank], t_ref[...], 1, 1).astype(BF)
    lhs = (seen[:rank], seen[rank:], dot(power[2 * rank :], c_ref[...], 1, 1).astype(BF))
    values = [dot(lhs[m], y_ref[:, m * units : (m + 1) * units]) for m in range(3)]

    def start():
        for m in range(3):
            total[m] = values[m]

    def finish():
        rows = dot(power, picked(place_ref, power.shape[1], e_ref.shape[0])).astype(BF)
        error = (e_ref[...].astype(F32) + e_other_ref[...].astype(F32)).astype(BF)
        for m in range(3):
            value = (values[m] + total[m]) * scale
            value = value + dot(
                rows[m * rank : (m + 1) * rank], error[:, m * units : (m + 1) * units]
            )
            value = (value * (1.0 / groups)).astype(BF)
            step = units // 4
            for i in range(4):
                out_ref[i, m * rank : (m + 1) * rank] = value[:, i * step : (i + 1) * step]

    pl.when(pl.program_id(0) == 0)(start)
    pl.when(pl.program_id(0) == 1)(finish)


def factor_body(place_ref, p_ref, inverse_ref, hats_ref):
    power = stacked(p_ref)
    r = power.shape[0] // 3
    low = power.astype(BF)
    gram = jnp.stack(
        [dot(low[m * r : (m + 1) * r], low[m * r : (m + 1) * r], 1, 1) for m in range(3)]
    )
    rows = lax.broadcasted_iota(jnp.int32, (3, r, 2 * r), 1)
    cols = lax.broadcasted_iota(jnp.int32, (3, r, 2 * r), 2)
    both = jnp.concatenate([gram, jnp.zeros((3, r, r), F32)], axis=2)
    both = both + jnp.where(cols == rows + r, 1.0, 0.0)
    for j in range(r):
        column = jnp.where(rows[:, :, :1] > j, both[:, :, j : j + 1], 0.0)
        row = both[:, j : j + 1, :] / both[:, j : j + 1, j : j + 1]
        both = both - column * row
    diagonal = jnp.sum(jnp.where(cols == rows, both, 0.0), axis=2, keepdims=True)
    inverse = both[:, :, r:] * (1.0 / jnp.sqrt(diagonal))
    inverse_ref[...] = inverse
    mine = dot(low, picked(place_ref, low.shape[1], hats_ref.shape[2]))
    for m in range(3):
        hats_ref[m] = dot(inverse[m], mine[m * r : (m + 1) * r], 1, 0, HIGH)


def final_body(scale, core_ref, b_ref, inverse_ref, hats_ref, kept_ref, sent_ref, e_ref, err_ref, q_ref):
    r = inverse_ref.shape[1]
    units = q_ref.shape[2]
    half = units // 2
    core = core_ref[16]
    for m in range(3):
        right = jnp.concatenate(
            [b_ref[i, m * r : (m + 1) * r].astype(F32) for i in range(b_ref.shape[0])], axis=1
        )
        q_t = dot(inverse_ref[m], right, 1, 0, HIGH)
        q_ref[m] = q_t
        rebuilt = dot(hats_ref[m].astype(BF), q_t.astype(BF), 0, 0)
        kept = kept_ref[:, m * half : (m + 1) * half].astype(F32)
        sent = sent_ref[:, m * half : (m + 1) * half].astype(F32)
        for side in range(2):
            at = slice(m * units + side * half, m * units + (side + 1) * half)
            grad = jnp.where(core == side, kept, sent)
            value = grad * scale + e_ref[:, at].astype(F32)
            err_ref[0, :, at] = (value - rebuilt[:, side * half : (side + 1) * half]).astype(BF)


def token_body(order_ref, y_ref, *refs):
    own_ref, other_ref = refs[-2:]
    rows, tok = own_ref.shape[1:]
    wide = y_ref.shape[1] // 3 * 2
    for s in range(0, own_ref.shape[0], 2):
        value = dot(refs[s // 2][:, :wide], y_ref[:, :wide], 1, 1).astype(BF)
        for i in range(2):
            at = order_ref[s + i]
            own_ref[at] = value[i * rows : (i + 1) * rows, :tok]
            other_ref[at] = value[i * rows : (i + 1) * rows, tok:]


def turn_body(a_ref, b_ref, out_ref):
    value = a_ref[...].astype(F32) + b_ref[...].astype(F32)
    out_ref[...] = value.T.astype(BF)


def on_device(tokens, cotangent, gate_weight, up_weight, down_weight_t, error_memory, q_init):
    yi, xi, core = lax.axis_index(Y), lax.axis_index(X), lax.axis_index(C)
    rows, units = gate_weight.shape
    node_count, groups = lax.axis_size(NODE), lax.axis_size(GRP)
    half, rank = units // 2, q_init.shape[-1]
    tok, width = tokens.shape
    grad_scale = 1.0 / math.sqrt(tok * node_count)

    def first(value, by):
        return neighbour(value, 0, by)

    def second(value, by):
        return neighbour(value, 1, by)

    over, along = jnp.arange(4)[:, None], jnp.arange(4)[None, :]
    ys = jnp.where(core == 0, yi + over, yi + along) % 4
    xs = jnp.where(core == 0, xi + along, xi + over) % 4
    place = jnp.concatenate(
        [(ys * 4 + xs).reshape(-1), core.reshape(1), ((yi * 4 + xi) * rows).reshape(1)]
    ).astype(jnp.int32)

    wide = 3 * half
    error = error_memory[0]
    weights = [
        pltpu.with_memory_space_constraint(w, pltpu.HBM)
        for w in (gate_weight, up_weight, down_weight_t)
    ]
    own = call(start_body, struct((rows, wide)), ins=[SCALAR] + [WHOLE] * 3, vmem=3)(place, *weights)
    from_left, from_right = first(own, 1), first(own, -1)
    other_t, other_c = other_core(tokens), other_core(cotangent)
    e_mine, e_send = call(
        error_body, (struct((rows, wide)),) * 2, ins=[SCALAR, WHOLE], vmem=3
    )(place, error)
    e_other = other_core(e_send)
    t_roll, t_both = rolled(place, tokens, other_t, rows)
    from_left, from_right, t_roll = lax.optimization_barrier((from_left, from_right, t_roll))
    at = rows // 32 * 16
    low, far_low, far_high = call(
        low_body,
        (struct((2 * rows, wide)), struct((at, wide)), struct((rows - at, wide))),
        vmem=2,
    )(own, from_left, from_right)
    far_low, far_high = first(far_low, 1), first(far_high, -1)
    left_low, right_low = second(low, 1), second(low, -1)
    c_roll, c_both = rolled(place, cotangent, other_c, rows)
    high = call(high_body, struct((2 * rows, wide)), vmem=2)(far_low, far_high, from_left)
    left_high = second(high, 1)
    right_high = second(high, -1)
    over_low, over_high = second(left_low, 1), second(right_high, -1)
    q_rows = lax.dynamic_slice_in_dim(jnp.swapaxes(q_init, 1, 2), core * half, half, 2).astype(BF)

    partial = ahead(((0, 0), (0, 1)), t_roll, c_roll, (low, high))
    slots = ((3, 0), (1, 0), (3, 1), (1, 1))
    partial = ahead(slots, t_roll, c_roll, (left_low, right_low, left_high, right_high), partial)
    long, mine = (4 * rows, wide), (groups, 3 * rank // groups, width)
    block = pl.BlockSpec((tok, wide), lambda k: (k, 0))

    def slot(b):
        return pl.BlockSpec((4, 1, rows, tok), lambda k: (0, b, 0, k))

    def fixed(*shape):
        return pl.BlockSpec(shape, lambda k: (0,) * len(shape))

    grads, far_own, far_other, power = call(
        functools.partial(late_body, grad_scale, groups),
        (far_struct((2 * tok, wide)), far_struct(long), far_struct(long), far_struct(mine)),
        grid=(2,),
        ins=[SCALAR] + [WHOLE] * 10,
        outs=(block, fixed(*long), fixed(*long), fixed(*mine)),
        scratch=[pltpu.VMEM((3 * rank, width), F32)],
        flops=2 * 2 * tok * 8 * rows * wide,
        vmem=16,
    )(
        place, *near(partial, t_roll, c_roll), over_low, over_high, q_rows, *near(t_both, c_both),
        e_mine, e_other,
    )

    four = (4, 4, rows, 2 * tok)
    rolls = far(t_roll.reshape(four), c_roll.reshape(four))
    one_own, one_other, three_own, three_other = call(
        near_body,
        (far_struct(long),) * 4,
        grid=(2,),
        ins=[slot(1), slot(1), slot(3), slot(3), block],
        outs=(fixed(*long),) * 4,
        flops=2 * 2 * tok * 8 * rows * wide,
        vmem=16,
    )(*rolls, *rolls, *far(grads))

    power = spread(exchange(power, GRP), node_count)
    power, one_other, three_own = lax.optimization_barrier((power, one_other, three_own))
    power = spread(exchange(power, NODE), groups)
    power = exchange(power, GRP)

    def relay(send, away_own, away_other, one_own, one_other, three_own, three_other):
        to_right, to_left = send(away_own, 1), send(away_other, -1)
        left_other, right_own = send(one_other, 1), send(three_own, -1)
        left_own = send((one_own.astype(F32) + to_right.astype(F32)).astype(BF), 1)
        right_other = send((three_other.astype(F32) + to_left.astype(F32)).astype(BF), -1)
        return right_own, right_other, left_own, left_other

    terms = relay(first, far_own, far_other, one_own, one_other, three_own, three_other)
    sums = call(
        home_body,
        (far_struct((rows, wide)),) * 8,
        grid=(2,),
        ins=[slot(0), slot(0), block] + [fixed(*long)] * 4,
        outs=(fixed(rows, wide),) * 8,
        flops=2 * 2 * tok * 4 * rows * wide,
        vmem=16,
    )(*rolls, *far(grads), *far(*terms))
    own_sums, other_sums = sums[:4], sums[4:]
    right_own, right_other, left_own, left_other = relay(
        second, own_sums[2], other_sums[2], own_sums[1], other_sums[1], own_sums[3], other_sums[3]
    )

    def total(value, a, b):
        return (value.astype(F32) + a.astype(F32) + b.astype(F32)).astype(BF)

    kept = total(own_sums[0], right_own, left_own)
    sent = other_core(total(other_sums[0], right_other, left_other))

    tiles = call(
        functools.partial(right_body, grad_scale, groups),
        struct((4, 3 * rank, half // 4)),
        grid=(2,),
        ins=[SCALAR, WHOLE] + [pl.BlockSpec((tok, width), lambda k: (k, 0))] * 2 + [block, WHOLE, WHOLE],
        outs=fixed(4, 3 * rank, half // 4),
        scratch=[pltpu.VMEM((3, rank, half), F32)],
        flops=4 * 3 * rank * 2 * tok * width,
        vmem=12,
    )(place, power, *far(t_both, c_both, grads), e_mine, e_other)
    tiles = spread(exchange(tiles, Z), node_count)
    tiles = spread(exchange(tiles, NODE), groups)
    tiles = exchange(tiles, (C, Z))
    inverse, hats = call(
        factor_body,
        (struct((3, rank, rank), F32), struct((3, rank, rows), F32)),
        ins=[SCALAR, WHOLE],
        flops=1 << 24,
        vmem=2,
    )(place, power)

    pieces = (low, high, right_low, right_high, over_low, over_high, left_low, left_high)
    token_own, token_other = call(
        token_body,
        (struct((node_count, rows, tok)),) * 2,
        ins=[SCALAR] + [WHOLE] * 9,
        flops=2 * 2 * tok * width * 2 * half,
        vmem=12,
    )(place, *far(grads, *pieces))
    token_grad = call(turn_body, struct((tok, width)), vmem=4)(
        token_own.reshape(width, tok), other_core(token_other).reshape(width, tok)
    )

    new_error, q_new = call(
        functools.partial(final_body, grad_scale),
        (struct((1, rows, 3 * units)), struct((3, rank, units), F32)),
        ins=[SCALAR] + [WHOLE] * 6,
        vmem=3,
    )(place, tiles, inverse, hats, kept, sent, error)
    return (token_grad, new_error, jnp.swapaxes(hats, 1, 2), jnp.swapaxes(q_new, 1, 2))


def solution(mesh):
    finer = Mesh(mesh.devices.reshape(4, 4, 4, 2), NODE_GRP)
    placed = (
        P(NODE_GRP, None),
        P(NODE_GRP, None),
        P(NODE, None),
        P(NODE, None),
        P(NODE, None),
        P(GRP, NODE, None),
        P(),
    )

    return jax.shard_map(
        on_device,
        mesh=finer,
        in_specs=placed,
        out_specs=(P(NODE_GRP, None), P(GRP, NODE, None), P(None, NODE, None), P()),
        check_vma=False,
    )
```

profile of v0, /device:TPU:1, one launch (start us, length us, event | category | flops | bytes accessed | tf_op | source)
XLA Modules:
  0.0 205.2 jit_solution(7154628280154782285)
XLA Ops:
  0.6 1.5 collective-permute-start.2
  2.5 1.2 shard_map.102.own_ref
  3.7 2.9 %collective-permute-start.1 = (bf16[112,1536]{1,0:T(8,128)(2,1)S(1)}, bf16[112,1536]{1,0:T(8,128)(2,1)S(1)}, u32[]{:S(2)}, u32[]{:S(2)}) collective-permute-start(bf16[112,1536]{1,0:T(8,128)(2,1)S(1)} %shard_map.102.own_ref), channel_id=1, source_target_pairs={{0,24},{1,97},{2,26},{3,99},{4,28},{5,101},{6,30},{7,103},{8,0},{9... | collective-permute-start | bytes 1032200 | tf_op jit(solution)/shard_map/ppermute | solution.py:30
  6.6 1.1 copy-done.11
  7.7 1.3 copy-done.9
  9.1 1.3 copy-done.12
  10.4 1.7 shard_map.103
  12.1 1.5 copy-done.4
  14.2 1.2 shard_map.105
  15.4 2.0 collective-permute-start.7
  17.4 1.1 collective-permute-start.4
  18.5 4.8 %collective-permute-done.6.far_low_ref = bf16[48,1536]{1,0:T(8,128)(2,1)S(1)} collective-permute-done((bf16[48,1536]{1,0:T(8,128)(2,1)S(1)}, bf16[48,1536]{1,0:T(8,128)(2,1)S(1)}, u32[]{:S(2)}, u32[]{:S(2)}) %collective-permute-start.6) | collective-permute-done | bytes 147488 | tf_op jit(solution)/shard_map/ppermute | solution.py:30
  24.2 3.1 %collective-permute-start.9 = (bf16[224,1536]{1,0:T(8,128)(2,1)}, bf16[224,1536]{1,0:T(8,128)(2,1)}, u32[]{:S(2)}, u32[]{:S(2)}) collective-permute-start(bf16[224,1536]{1,0:T(8,128)(2,1)} %shard_map.106.refs_1_), channel_id=1, source_target_pairs={{0,96},{1,25},{2,98},{3,27},{4,100},{5,29},{6,102},{7,31},{8,104},... | collective-permute-start | bytes 2064392 | tf_op jit(solution)/shard_map/ppermute | solution.py:30
  28.7 1.9 collective-permute-done.4.refs_0_.refs_6_
  30.6 4.9 %collective-permute-done.9.refs_3_ = bf16[224,1536]{1,0:T(8,128)(2,1)} collective-permute-done((bf16[224,1536]{1,0:T(8,128)(2,1)}, bf16[224,1536]{1,0:T(8,128)(2,1)}, u32[]{:S(2)}, u32[]{:S(2)}) %collective-permute-start.9) | collective-permute-done | bytes 688160 | tf_op jit(solution)/shard_map/ppermute | solution.py:30
  35.5 3.4 %collective-permute-start.11 = (bf16[224,1536]{1,0:T(8,128)(2,1)}, bf16[224,1536]{1,0:T(8,128)(2,1)}, u32[]{:S(2)}, u32[]{:S(2)}) collective-permute-start(bf16[224,1536]{1,0:T(8,128)(2,1)} %collective-permute-done.9.refs_3_), channel_id=1, source_target_pairs={{0,96},{1,25},{2,98},{3,27},{4,100},{5,29},{6,102},{7,31},{8,104},... | collective-permute-start | bytes 2064392 | tf_op jit(solution)/shard_map/ppermute | solution.py:30
  38.9 1.1 copy-done.7
  41.3 3.3 %collective-permute-start.12 = (bf16[112,1536]{1,0:T(8,128)(2,1)}, bf16[112,1536]{1,0:T(8,128)(2,1)S(1)}, u32[]{:S(2)}, u32[]{:S(2)}) collective-permute-start(bf16[112,1536]{1,0:T(8,128)(2,1)} %copy-done.16), channel_id=1, source_target_pairs={{0,1},{1,0},{2,3},{3,2},{4,5},{5,4},{6,7},{7,6},{8,9},{9,8},{10,11... | collective-permute-start | bytes 1032200 | tf_op jit(solution)/shard_map/ppermute | solution.py:34
  44.7 1.3 copy-done.10
  46.0 2.5 %shard_map.104 = (bf16[16,112,768]{2,1,0:T(8,128)(2,1)S(1)}, bf16[768,1792]{1,0:T(8,128)(2,1)S(1)}) custom-call(s32[18]{0:T(128)S(1)} %pad_add_fusion.place_ref.order_ref.core_ref, bf16[384,1792]{1,0:T(8,128)(2,1)S(1)} %copy-done.10, bf16[384,1792]{1,0:T(8,128)(2,1)} %collective-permute-done.3.other_ref), custom_call_target="tpu_custom_call" | custom-call | tf_op jit(solution)/shard_map/pallas_call | solution.py:151
  48.5 4.0 %shard_map.107.refs_4_ = f32[768,1536]{1,0:T(8,128)S(1)} custom-call(bf16[16,112,768]{2,1,0:T(8,128)(2,1)S(1)} %get-tuple-element.42.t_ref, bf16[16,112,768]{2,1,0:T(8,128)(2,1)S(1)} %get-tuple-element.43.c_ref, bf16[224,1536]{1,0:T(8,128)(2,1)} %get-tuple-element.46.refs_0_, bf16[224,1536]{1,0:T(8,128)(2,1)} %shard_map.106.refs_1_), custom_call_target="tpu_custom_call" | custom-call | flops 1056964608 | bytes 1048576 | tf_op jit(solution)/shard_map/pallas_call | solution.py:198
  52.6 4.9 %shard_map.108.part_all = f32[768,1536]{1,0:T(8,128)S(1)} custom-call(bf16[16,112,768]{2,1,0:T(8,128)(2,1)S(1)} %get-tuple-element.42.t_ref, bf16[16,112,768]{2,1,0:T(8,128)(2,1)S(1)} %get-tuple-element.43.c_ref, bf16[224,1536]{1,0:T(8,128)(2,1)} %collective-permute-done.4.refs_0_.refs_6_, bf16[224,1536]{1,0:T(8,128)(2,1)} %collective-permute-done.5.refs_1_.refs_2_, ...), custom_call_target="tpu_custom_call" | custom-call | flops 2113929216 | bytes 1048576 | tf_op jit(solution)/shard_map/pallas_call | solution.py:198
  57.5 10.2 %shard_map.110 = (bf16[768,1536]{1,0:T(8,128)(2,1)}, bf16[448,1536]{1,0:T(8,128)(2,1)}, bf16[448,1536]{1,0:T(8,128)(2,1)}, bf16[8,12,1792]{2,1,0:T(8,128)(2,1)}) custom-call(s32[18]{0:T(128)S(1)} %pad_add_fusion.place_ref.order_ref.core_ref, f32[768,1536]{1,0:T(8,128)S(1)} %shard_map.108.part_all, bf16[16,112,768]{2,1,0:T(8,128)(2,1)S(1)} %get-tuple-element.42.t_ref, ...), custom_call_target="tpu_custom_call" | custom-call | flops 2113929216 | bytes 1048576 | tf_op jit(solution)/shard_map/pallas_call | solution.py:460
  67.8 1.5 collective-permute-start.17
  69.3 5.9 %all-to-all-start = ((bf16[8,12,1792]{2,1,0:T(8,128)(2,1)}), bf16[8,12,1792]{2,1,0:T(8,128)(2,1)S(1)}, u32[]{:S(2)}, u32[]{:S(2)}) async-start(bf16[8,12,1792]{2,1,0:T(8,128)(2,1)} %get-tuple-element.56), calls=%async_computation | async-start | bytes 917504 | tf_op jit(solution)/shard_map/all_to_all | solution.py:38
  75.1 7.8 %shard_map.114 = (bf16[448,1536]{1,0:T(8,128)(2,1)}, bf16[448,1536]{1,0:T(8,128)(2,1)}, bf16[448,1536]{1,0:T(8,128)(2,1)}, bf16[448,1536]{1,0:T(8,128)(2,1)}) custom-call(bf16[4,4,112,768]{3,2,1,0:T(8,128)(2,1)} %bitcast.11, bf16[4,4,112,768]{3,2,1,0:T(8,128)(2,1)} %bitcast.14, bf16[4,4,112,768]{3,2,1,0:T(8,128)(2,1)} %bitcast.12, ...), custom_call_target="tpu_custom_call" | custom-call | flops 2113929216 | bytes 1048576 | tf_op jit(solution)/shard_map/pallas_call | solution.py:476
  86.3 2.9 %add_convert_fusion.1 = bf16[448,1536]{1,0:T(8,128)(2,1)} fusion(bf16[448,1536]{1,0:T(8,128)(2,1)} %collective-permute-done.15, bf16[448,1536]{1,0:T(8,128)(2,1)S(1)} %copy-done.18), kind=kLoop, calls=%fused_computation.1 | loop fusion | flops 2752512 | bytes 4128768 | tf_op jit(solution)/shard_map/convert_element_type | solution.py:495
  89.2 2.0 collective-permute-start.16
  91.3 1.4 add_convert_fusion
  92.7 4.1 %all-to-all-start.1 = ((bf16[16,12,1792]{2,1,0:T(8,128)(2,1)}), bf16[16,12,1792]{2,1,0:T(8,128)(2,1)S(1)}, u32[]{:S(2)}, u32[]{:S(2)}) async-start(bf16[16,12,1792]{2,1,0:T(8,128)(2,1)} %shard_map.113), calls=%async_computation.1 | async-start | bytes 1835008 | tf_op jit(solution)/shard_map/all_to_all | solution.py:38
  96.8 8.1 %shard_map.111 = (bf16[16,112,384]{2,1,0:T(8,128)(2,1)S(1)}, bf16[16,112,384]{2,1,0:T(8,128)(2,1)}) custom-call(s32[18]{0:T(128)S(1)} %pad_add_fusion.place_ref.order_ref.core_ref, bf16[768,1536]{1,0:T(8,128)(2,1)} %get-tuple-element.53.y_ref.grads_ref, bf16[224,1536]{1,0:T(8,128)(2,1)} %get-tuple-element.46.refs_0_, bf16[224,1536]{1,0:T(8,128)(2,1)} %shard_map.106.refs_1_, ...), custom_call_target="tpu_custom_call" | custom-call | flops 2818572288 | bytes 1048576 | tf_op jit(solution)/shard_map/pallas_call | solution.py:541
  104.9 2.6 %collective-permute-start.13 = (bf16[16,112,384]{2,1,0:T(8,128)(2,1)}, bf16[16,112,384]{2,1,0:T(8,128)(2,1)}, u32[]{:S(2)}, u32[]{:S(2)}) collective-permute-start(bf16[16,112,384]{2,1,0:T(8,128)(2,1)} %get-tuple-element.55), channel_id=1, source_target_pairs={{0,1},{1,0},{2,3},{3,2},{4,5},{5,4},{6,7},{7,6},{8,9},{9,8},{10,11... | collective-permute-start | bytes 4128776 | tf_op jit(solution)/shard_map/ppermute | solution.py:34
  107.5 19.9 %all-to-all-done.1.in_ref = bf16[16,12,1792]{2,1,0:T(8,128)(2,1)S(1)} async-done(((bf16[16,12,1792]{2,1,0:T(8,128)(2,1)}), bf16[16,12,1792]{2,1,0:T(8,128)(2,1)S(1)}, u32[]{:S(2)}, u32[]{:S(2)}) %all-to-all-start.1) | async-done | bytes 688160 | tf_op jit(solution)/shard_map/all_to_all | solution.py:38
  128.3 16.1 %all_to_all.30.p_ref = bf16[8,12,1792]{2,1,0:T(8,128)(2,1)S(1)} all-to-all(bf16[8,12,1792]{2,1,0:T(8,128)(2,1)} %shard_map.115), channel_id=1, replica_groups=mesh['node_0'=4,'node_1'=4,'grp_0'=4,'grp_1'=2] {'grp_0','grp_1'}, dimensions={0} | all-to-all | bytes 688128 | tf_op jit(solution)/shard_map/all_to_all | solution.py:38
  144.3 4.8 %shard_map.116 = bf16[4,96,128]{2,1,0:T(8,128)(2,1)S(1)} custom-call(s32[18]{0:T(128)S(1)} %pad_add_fusion.place_ref.order_ref.core_ref, bf16[8,12,1792]{2,1,0:T(8,128)(2,1)S(1)} %all_to_all.30.p_ref, bf16[768,1792]{1,0:T(8,128)(2,1)} %copy-done.4, bf16[768,1792]{1,0:T(8,128)(2,1)} %copy-done.6, bf16[768,1536]{1,0:T(8,128)(2,1)} %get-tuple-element.53.y_ref.grads_ref, ...), custom_call_target="tpu_custom_call" | custom-call | flops 528482304 | bytes 1048576 | tf_op jit(solution)/shard_map/pallas_call | solution.py:519
  149.2 7.0 %all_to_all.31.in_ref = bf16[4,96,128]{2,1,0:T(8,128)(2,1)S(1)} all-to-all(bf16[4,96,128]{2,1,0:T(8,128)(2,1)S(1)} %shard_map.116), channel_id=1, replica_groups=mesh['node_0'=4,'node_1'=4,'grp_0'=4,'grp_1'=2] {'grp_0'}, dimensions={0} | all-to-all | bytes 196608 | tf_op jit(solution)/shard_map/all_to_all | solution.py:38
  157.0 3.6 %all-to-all-start.4 = ((bf16[16,96,128]{2,1,0:T(8,128)(2,1)}), bf16[16,96,128]{2,1,0:T(8,128)(2,1)S(1)}, u32[]{:S(2)}, u32[]{:S(2)}) async-start(bf16[16,96,128]{2,1,0:T(8,128)(2,1)} %shard_map.117), calls=%async_computation.4 | async-start | bytes 786432 | tf_op jit(solution)/shard_map/all_to_all | solution.py:38
  160.6 7.4 %shard_map.120 = (bf16[112,1536]{1,0:T(8,128)(2,1)}, bf16[112,1536]{1,0:T(8,128)(2,1)}, bf16[112,1536]{1,0:T(8,128)(2,1)}, bf16[112,1536]{1,0:T(8,128)(2,1)}, bf...) custom-call(bf16[4,4,112,768]{3,2,1,0:T(8,128)(2,1)} %bitcast.13, ...), custom_call_target="tpu_custom_call" | custom-call | flops 1056964608 | bytes 1048576 | tf_op jit(solution)/shard_map/pallas_call | solution.py:499
  168.0 2.5 %collective-permute-start.23 = (bf16[112,1536]{1,0:T(8,128)(2,1)}, bf16[112,1536]{1,0:T(8,128)(2,1)S(1)}, u32[]{:S(2)}, u32[]{:S(2)}) collective-permute-start(bf16[112,1536]{1,0:T(8,128)(2,1)} %get-tuple-element.74), channel_id=1, source_target_pairs={{0,96},{1,25},{2,98},{3,27},{4,100},{5,29},{6,102},{7,31},{8,104},... | collective-permute-start | bytes 1032200 | tf_op jit(solution)/shard_map/ppermute | solution.py:30
  170.5 4.4 %shard_map.119 = (f32[3,32,32]{2,1,0:T(8,128)S(1)}, f32[3,32,112]{2,1,0:T(8,128)}) custom-call(s32[18]{0:T(128)S(1)} %pad_add_fusion.place_ref.order_ref.core_ref, bf16[8,12,1792]{2,1,0:T(8,128)(2,1)S(1)} %all_to_all.30.p_ref), custom_call_target="tpu_custom_call" | custom-call | flops 16777216 | bytes 1048576 | tf_op jit(solution)/shard_map/pallas_call | solution.py:532
  174.9 3.0 %shard_map.112 = bf16[384,1792]{1,0:T(8,128)(2,1)} custom-call(bf16[1792,384]{1,0:T(8,128)(2,1)S(1)} %bitcast.19, bf16[1792,384]{1,0:T(8,128)(2,1)} %bitcast.5.b_ref), custom_call_target="tpu_custom_call" | custom-call | tf_op jit(solution)/shard_map/pallas_call | solution.py:548
  178.7 6.2 %all-to-all-start.5 = ((bf16[8,96,128]{2,1,0:T(8,128)(2,1)}), bf16[8,96,128]{2,1,0:T(8,128)(2,1)S(1)}, u32[]{:S(2)}, u32[]{:S(2)}) async-start(bf16[8,96,128]{2,1,0:T(8,128)(2,1)} %shard_map.118), calls=%async_computation.5 | async-start | bytes 393216 | tf_op jit(solution)/shard_map/all_to_all | solution.py:38
  184.8 2.4 %collective-permute-start.20 = (bf16[112,1536]{1,0:T(8,128)(2,1)S(1)}, bf16[112,1536]{1,0:T(8,128)(2,1)S(1)}, u32[]{:S(2)}, u32[]{:S(2)}) collective-permute-start(bf16[112,1536]{1,0:T(8,128)(2,1)S(1)} %copy-done.23), channel_id=1, source_target_pairs={{0,96},{1,25},{2,98},{3,27},{4,100},{5,29},{6,102},{7,31},{8,104},... | collective-permute-start | bytes 1032200 | tf_op jit(solution)/shard_map/ppermute | solution.py:30
  187.6 2.5 %collective-permute-start.24 = (bf16[112,1536]{1,0:T(8,128)(2,1)S(1)}, bf16[112,1536]{1,0:T(8,128)(2,1)S(1)}, u32[]{:S(2)}, u32[]{:S(2)}) collective-permute-start(bf16[112,1536]{1,0:T(8,128)(2,1)S(1)} %add_convert_fusion.3), channel_id=1, source_target_pairs={{0,96},{1,25},{2,98},{3,27},{4,100},{5,29},{6,102},{7,31},{8,104},... | collective-permute-start | bytes 1032200 | tf_op jit(solution)/shard_map/ppermute | solution.py:30
  190.1 4.9 %collective-permute-done.21 = bf16[112,1536]{1,0:T(8,128)(2,1)S(1)} collective-permute-done((bf16[112,1536]{1,0:T(8,128)(2,1)}, bf16[112,1536]{1,0:T(8,128)(2,1)S(1)}, u32[]{:S(2)}, u32[]{:S(2)}) %collective-permute-start.21) | collective-permute-done | bytes 344096 | tf_op jit(solution)/shard_map/ppermute | solution.py:30
  195.2 3.2 %collective-permute-done.25 = bf16[112,1536]{1,0:T(8,128)(2,1)S(1)} collective-permute-done((bf16[112,1536]{1,0:T(8,128)(2,1)}, bf16[112,1536]{1,0:T(8,128)(2,1)S(1)}, u32[]{:S(2)}, u32[]{:S(2)}) %collective-permute-start.25) | collective-permute-done | bytes 344096 | tf_op jit(solution)/shard_map/ppermute | solution.py:30
  198.7 4.0 %collective-permute-done.22 = bf16[112,1536]{1,0:T(8,128)(2,1)S(1)} collective-permute-done((bf16[112,1536]{1,0:T(8,128)(2,1)S(1)}, bf16[112,1536]{1,0:T(8,128)(2,1)S(1)}, u32[]{:S(2)}, u32[]{:S(2)}) %collective-permute-start.22) | collective-permute-done | bytes 344096 | tf_op jit(solution)/shard_map/ppermute | solution.py:30
  202.9 2.3 %shard_map.121 = (bf16[1,112,3072]{2,1,0:T(8,128)(2,1)}, f32[3,32,1024]{2,1,0:T(8,128)}) custom-call(s32[18]{0:T(128)S(1)} %pad_add_fusion.place_ref.order_ref.core_ref, bf16[8,96,128]{2,1,0:T(8,128)(2,1)S(1)} %all-to-all-done.5.b_ref, f32[3,32,32]{2,1,0:T(8,128)S(1)} %get-tuple-element.60.inverse_ref, f32[3,32,112]{2,1,0:T(8,128)S(1)} %copy-done.15, ...), custom_call_target="tpu_custom_call" | custom-call | tf_op jit(solution)/shard_map/pallas_call | solution.py:552
  (98 shorter events, 11.4 us)
Async XLA Ops:
  0.6 44.0 %copy-start = (f32[3,1024,32]{1,2,0:T(8,128)S(1)}, f32[3,1024,32]{1,2,0:T(8,128)}, u32[]{:S(2)}) copy-start(f32[3,1024,32]{1,2,0:T(8,128)} %param.13) | copy-start | bytes 1179652
  0.6 6.0 %collective-permute-start.2 = (bf16[384,1792]{1,0:T(8,128)(2,1)}, bf16[384,1792]{1,0:T(8,128)(2,1)S(1)}, u32[]{:S(2)}, u32[]{:S(2)}) collective-permute-start(bf16[384,1792]{1,0:T(8,128)(2,1)} %own_ref.2), channel_id=1, source_target_pairs={{0,1},{1,0},{2,3},{3,2},{4,5},{5,4},{6,7},{7,6},{8,9},{9,8},{10,11... | collective-permute-start | bytes 4128776 | tf_op jit(solution)/shard_map/ppermute | solution.py:34
  3.7 10.0 %collective-permute-start.1 = (bf16[112,1536]{1,0:T(8,128)(2,1)S(1)}, bf16[112,1536]{1,0:T(8,128)(2,1)S(1)}, u32[]{:S(2)}, u32[]{:S(2)}) collective-permute-start(bf16[112,1536]{1,0:T(8,128)(2,1)S(1)} %shard_map.102.own_ref), channel_id=1, source_target_pairs={{0,24},{1,97},{2,26},{3,99},{4,28},{5,101},{6,30},{7,103},{8,0},{9... | collective-permute-start | bytes 1032200 | tf_op jit(solution)/shard_map/ppermute | solution.py:30
  6.6 7.6 %collective-permute-start = (bf16[112,1536]{1,0:T(8,128)(2,1)S(1)}, bf16[112,1536]{1,0:T(8,128)(2,1)S(1)}, u32[]{:S(2)}, u32[]{:S(2)}) collective-permute-start(bf16[112,1536]{1,0:T(8,128)(2,1)S(1)} %shard_map.102.own_ref), channel_id=1, source_target_pairs={{0,8},{1,33},{2,10},{3,35},{4,12},{5,37},{6,14},{7,39},{8,16},{9,4... | collective-permute-start | bytes 1032200 | tf_op jit(solution)/shard_map/ppermute | solution.py:30
  6.6 34.7 %collective-permute-start.3 = (bf16[384,1792]{1,0:T(8,128)(2,1)}, bf16[384,1792]{1,0:T(8,128)(2,1)}, u32[]{:S(2)}, u32[]{:S(2)}) collective-permute-start(bf16[384,1792]{1,0:T(8,128)(2,1)} %own_ref.3), channel_id=1, source_target_pairs={{0,1},{1,0},{2,3},{3,2},{4,5},{5,4},{6,7},{7,6},{8,9},{9,8},{10,11... | collective-permute-start | bytes 4128776 | tf_op jit(solution)/shard_map/ppermute | solution.py:34
  13.6 43.8 %copy-start.2 = (bf16[16,112,768]{2,1,0:T(8,128)(2,1)}, bf16[16,112,768]{2,1,0:T(8,128)(2,1)S(1)}, u32[]{:S(2)}) copy-start(bf16[16,112,768]{2,1,0:T(8,128)(2,1)S(1)} %get-tuple-element.42.t_ref) | copy-start | bytes 8257540
  15.4 7.9 %collective-permute-start.7 = (bf16[64,1536]{1,0:T(8,128)(2,1)S(1)}, bf16[64,1536]{1,0:T(8,128)(2,1)S(1)}, u32[]{:S(2)}, u32[]{:S(2)}) collective-permute-start(bf16[64,1536]{1,0:T(8,128)(2,1)S(1)} %get-tuple-element.48), channel_id=1, source_target_pairs={{0,24},{1,97},{2,26},{3,99},{4,28},{5,101},{6,30},{7,103},{8,0},{9... | collective-permute-start | bytes 589832 | tf_op jit(solution)/shard_map/ppermute | solution.py:30
  17.4 5.9 %collective-permute-start.6 = (bf16[48,1536]{1,0:T(8,128)(2,1)S(1)}, bf16[48,1536]{1,0:T(8,128)(2,1)S(1)}, u32[]{:S(2)}, u32[]{:S(2)}) collective-permute-start(bf16[48,1536]{1,0:T(8,128)(2,1)S(1)} %get-tuple-element.47), channel_id=1, source_target_pairs={{0,8},{1,33},{2,10},{3,35},{4,12},{5,37},{6,14},{7,39},{8,16},{9,4... | collective-permute-start | bytes 442376 | tf_op jit(solution)/shard_map/ppermute | solution.py:30
  17.4 13.2 %collective-permute-start.4 = (bf16[224,1536]{1,0:T(8,128)(2,1)}, bf16[224,1536]{1,0:T(8,128)(2,1)}, u32[]{:S(2)}, u32[]{:S(2)}) collective-permute-start(bf16[224,1536]{1,0:T(8,128)(2,1)} %get-tuple-element.46.refs_0_), channel_id=1, source_target_pairs={{0,32},{1,9},{2,34},{3,11},{4,36},{5,13},{6,38},{7,15},{8,40},{9,1... | collective-permute-start | bytes 2064392 | tf_op jit(solution)/shard_map/ppermute | solution.py:30
  24.2 11.3 %collective-permute-start.9 = (bf16[224,1536]{1,0:T(8,128)(2,1)}, bf16[224,1536]{1,0:T(8,128)(2,1)}, u32[]{:S(2)}, u32[]{:S(2)}) collective-permute-start(bf16[224,1536]{1,0:T(8,128)(2,1)} %shard_map.106.refs_1_), channel_id=1, source_target_pairs={{0,96},{1,25},{2,98},{3,27},{4,100},{5,29},{6,102},{7,31},{8,104},... | collective-permute-start | bytes 2064392 | tf_op jit(solution)/shard_map/ppermute | solution.py:30
  27.3 25.2 %collective-permute-start.5 = (bf16[224,1536]{1,0:T(8,128)(2,1)}, bf16[224,1536]{1,0:T(8,128)(2,1)}, u32[]{:S(2)}, u32[]{:S(2)}) collective-permute-start(bf16[224,1536]{1,0:T(8,128)(2,1)} %get-tuple-element.46.refs_0_), channel_id=1, source_target_pairs={{0,96},{1,25},{2,98},{3,27},{4,100},{5,29},{6,102},{7,31},{8,104},... | collective-permute-start | bytes 2064392 | tf_op jit(solution)/shard_map/ppermute | solution.py:30
  27.9 24.7 %collective-permute-start.8 = (bf16[224,1536]{1,0:T(8,128)(2,1)}, bf16[224,1536]{1,0:T(8,128)(2,1)}, u32[]{:S(2)}, u32[]{:S(2)}) collective-permute-start(bf16[224,1536]{1,0:T(8,128)(2,1)} %shard_map.106.refs_1_), channel_id=1, source_target_pairs={{0,32},{1,9},{2,34},{3,11},{4,36},{5,13},{6,38},{7,15},{8,40},{9,1... | collective-permute-start | bytes 2064392 | tf_op jit(solution)/shard_map/ppermute | solution.py:30
  30.6 26.9 %collective-permute-start.10 = (bf16[224,1536]{1,0:T(8,128)(2,1)}, bf16[224,1536]{1,0:T(8,128)(2,1)}, u32[]{:S(2)}, u32[]{:S(2)}) collective-permute-start(bf16[224,1536]{1,0:T(8,128)(2,1)} %collective-permute-done.4.refs_0_.refs_6_), channel_id=1, source_target_pairs={{0,32},{1,9},{2,34},{3,11},{4,36},{5,13},{6,38},{7,15},{8,40},{9,1... | collective-permute-start | bytes 2064392 | tf_op jit(solution)/shard_map/ppermute | solution.py:30
  35.5 22.0 %collective-permute-start.11 = (bf16[224,1536]{1,0:T(8,128)(2,1)}, bf16[224,1536]{1,0:T(8,128)(2,1)}, u32[]{:S(2)}, u32[]{:S(2)}) collective-permute-start(bf16[224,1536]{1,0:T(8,128)(2,1)} %collective-permute-done.9.refs_3_), channel_id=1, source_target_pairs={{0,96},{1,25},{2,98},{3,27},{4,100},{5,29},{6,102},{7,31},{8,104},... | collective-permute-start | bytes 2064392 | tf_op jit(solution)/shard_map/ppermute | solution.py:30
  41.3 16.1 %collective-permute-start.12 = (bf16[112,1536]{1,0:T(8,128)(2,1)}, bf16[112,1536]{1,0:T(8,128)(2,1)S(1)}, u32[]{:S(2)}, u32[]{:S(2)}) collective-permute-start(bf16[112,1536]{1,0:T(8,128)(2,1)} %copy-done.16), channel_id=1, source_target_pairs={{0,1},{1,0},{2,3},{3,2},{4,5},{5,4},{6,7},{7,6},{8,9},{9,8},{10,11... | collective-permute-start | bytes 1032200 | tf_op jit(solution)/shard_map/ppermute | solution.py:34
  48.5 9.0 %copy-start.3 = (bf16[16,112,768]{2,1,0:T(8,128)(2,1)}, bf16[16,112,768]{2,1,0:T(8,128)(2,1)S(1)}, u32[]{:S(2)}) copy-start(bf16[16,112,768]{2,1,0:T(8,128)(2,1)S(1)} %get-tuple-element.43.c_ref) | copy-start | bytes 8257540
  48.5 9.0 %copy-start.6 = (bf16[768,1792]{1,0:T(8,128)(2,1)}, bf16[768,1792]{1,0:T(8,128)(2,1)S(1)}, u32[]{:S(2)}) copy-start(bf16[768,1792]{1,0:T(8,128)(2,1)S(1)} %get-tuple-element.50.c_both.c_ref) | copy-start | bytes 8257540
  52.5 5.0 %copy-start.5 = (bf16[768,1792]{1,0:T(8,128)(2,1)S(1)}, bf16[768,1792]{1,0:T(8,128)(2,1)}, u32[]{:S(2)}) copy-start(bf16[768,1792]{1,0:T(8,128)(2,1)} %copy-done.4) | copy-start | bytes 8257540
  57.5 10.3 %copy-start.13 = (bf16[112,1536]{1,0:T(8,128)(2,1)}, bf16[112,1536]{1,0:T(8,128)(2,1)S(1)}, u32[]{:S(2)}) copy-start(bf16[112,1536]{1,0:T(8,128)(2,1)S(1)} %collective-permute-done.12.e_other_ref) | copy-start | bytes 1032196
  67.7 18.6 %collective-permute-start.15 = (bf16[448,1536]{1,0:T(8,128)(2,1)}, bf16[448,1536]{1,0:T(8,128)(2,1)}, u32[]{:S(2)}, u32[]{:S(2)}) collective-permute-start(bf16[448,1536]{1,0:T(8,128)(2,1)} %get-tuple-element.64), channel_id=1, source_target_pairs={{0,24},{1,97},{2,26},{3,99},{4,28},{5,101},{6,30},{7,103},{8,0},{9... | collective-permute-start | bytes 4128776 | tf_op jit(solution)/shard_map/ppermute | solution.py:30
  67.8 23.5 %collective-permute-start.17 = (bf16[448,1536]{1,0:T(8,128)(2,1)}, bf16[448,1536]{1,0:T(8,128)(2,1)S(1)}, u32[]{:S(2)}, u32[]{:S(2)}) collective-permute-start(bf16[448,1536]{1,0:T(8,128)(2,1)} %get-tuple-element.66), channel_id=1, source_target_pairs={{0,8},{1,33},{2,10},{3,35},{4,12},{5,37},{6,14},{7,39},{8,16},{9,4... | collective-permute-start | bytes 4128776 | tf_op jit(solution)/shard_map/ppermute | solution.py:30
  69.3 14.5 %all-to-all-start = ((bf16[8,12,1792]{2,1,0:T(8,128)(2,1)}), bf16[8,12,1792]{2,1,0:T(8,128)(2,1)S(1)}, u32[]{:S(2)}, u32[]{:S(2)}) async-start(bf16[8,12,1792]{2,1,0:T(8,128)(2,1)} %get-tuple-element.56), calls=%async_computation | async-start | bytes 917504 | tf_op jit(solution)/shard_map/all_to_all | solution.py:38
  83.8 2.5 %copy-start.18 = (bf16[448,1536]{1,0:T(8,128)(2,1)S(1)}, bf16[448,1536]{1,0:T(8,128)(2,1)}, u32[]{:S(2)}) copy-start(bf16[448,1536]{1,0:T(8,128)(2,1)} %get-tuple-element.63) | copy-start | bytes 4128772
  84.8 75.7 %collective-permute-start.14 = (bf16[448,1536]{1,0:T(8,128)(2,1)}, bf16[448,1536]{1,0:T(8,128)(2,1)}, u32[]{:S(2)}, u32[]{:S(2)}) collective-permute-start(bf16[448,1536]{1,0:T(8,128)(2,1)} %get-tuple-element.62), channel_id=1, source_target_pairs={{0,24},{1,97},{2,26},{3,99},{4,28},{5,101},{6,30},{7,103},{8,0},{9... | collective-permute-start | bytes 4128776 | tf_op jit(solution)/shard_map/ppermute | solution.py:30
  85.7 74.9 %collective-permute-start.19 = (bf16[448,1536]{1,0:T(8,128)(2,1)}, bf16[448,1536]{1,0:T(8,128)(2,1)}, u32[]{:S(2)}, u32[]{:S(2)}) collective-permute-start(bf16[448,1536]{1,0:T(8,128)(2,1)} %get-tuple-element.67), channel_id=1, source_target_pairs={{0,8},{1,33},{2,10},{3,35},{4,12},{5,37},{6,14},{7,39},{8,16},{9,4... | collective-permute-start | bytes 4128776 | tf_op jit(solution)/shard_map/ppermute | solution.py:30
  86.3 5.0 %copy-start.17 = (bf16[448,1536]{1,0:T(8,128)(2,1)S(1)}, bf16[448,1536]{1,0:T(8,128)(2,1)}, u32[]{:S(2)}) copy-start(bf16[448,1536]{1,0:T(8,128)(2,1)} %get-tuple-element.65) | copy-start | bytes 4128772
  89.2 71.3 %collective-permute-start.16 = (bf16[448,1536]{1,0:T(8,128)(2,1)}, bf16[448,1536]{1,0:T(8,128)(2,1)}, u32[]{:S(2)}, u32[]{:S(2)}) collective-permute-start(bf16[448,1536]{1,0:T(8,128)(2,1)} %add_convert_fusion.1), channel_id=1, source_target_pairs={{0,24},{1,97},{2,26},{3,99},{4,28},{5,101},{6,30},{7,103},{8,0},{9... | collective-permute-start | bytes 4128776 | tf_op jit(solution)/shard_map/ppermute | solution.py:30
  92.7 67.8 %collective-permute-start.18 = (bf16[448,1536]{1,0:T(8,128)(2,1)}, bf16[448,1536]{1,0:T(8,128)(2,1)}, u32[]{:S(2)}, u32[]{:S(2)}) collective-permute-start(bf16[448,1536]{1,0:T(8,128)(2,1)} %add_convert_fusion), channel_id=1, source_target_pairs={{0,8},{1,33},{2,10},{3,35},{4,12},{5,37},{6,14},{7,39},{8,16},{9,4... | collective-permute-start | bytes 4128776 | tf_op jit(solution)/shard_map/ppermute | solution.py:30
  92.7 34.6 %all-to-all-start.1 = ((bf16[16,12,1792]{2,1,0:T(8,128)(2,1)}), bf16[16,12,1792]{2,1,0:T(8,128)(2,1)S(1)}, u32[]{:S(2)}, u32[]{:S(2)}) async-start(bf16[16,12,1792]{2,1,0:T(8,128)(2,1)} %shard_map.113), calls=%async_computation.1 | async-start | bytes 1835008 | tf_op jit(solution)/shard_map/all_to_all | solution.py:38
  104.9 39.4 %copy-start.14 = (bf16[112,1536]{1,0:T(8,128)(2,1)S(1)}, bf16[112,1536]{1,0:T(8,128)(2,1)}, u32[]{:S(2)}) copy-start(bf16[112,1536]{1,0:T(8,128)(2,1)} %copy-done.13) | copy-start | bytes 1032196
  104.9 69.9 %collective-permute-start.13 = (bf16[16,112,384]{2,1,0:T(8,128)(2,1)}, bf16[16,112,384]{2,1,0:T(8,128)(2,1)}, u32[]{:S(2)}, u32[]{:S(2)}) collective-permute-start(bf16[16,112,384]{2,1,0:T(8,128)(2,1)} %get-tuple-element.55), channel_id=1, source_target_pairs={{0,1},{1,0},{2,3},{3,2},{4,5},{5,4},{6,7},{7,6},{8,9},{9,8},{10,11... | collective-permute-start | bytes 4128776 | tf_op jit(solution)/shard_map/ppermute | solution.py:34
  157.0 20.9 %all-to-all-start.4 = ((bf16[16,96,128]{2,1,0:T(8,128)(2,1)}), bf16[16,96,128]{2,1,0:T(8,128)(2,1)S(1)}, u32[]{:S(2)}, u32[]{:S(2)}) async-start(bf16[16,96,128]{2,1,0:T(8,128)(2,1)} %shard_map.117), calls=%async_computation.4 | async-start | bytes 786432 | tf_op jit(solution)/shard_map/all_to_all | solution.py:38
  168.0 19.5 %collective-permute-start.23 = (bf16[112,1536]{1,0:T(8,128)(2,1)}, bf16[112,1536]{1,0:T(8,128)(2,1)S(1)}, u32[]{:S(2)}, u32[]{:S(2)}) collective-permute-start(bf16[112,1536]{1,0:T(8,128)(2,1)} %get-tuple-element.74), channel_id=1, source_target_pairs={{0,96},{1,25},{2,98},{3,27},{4,100},{5,29},{6,102},{7,31},{8,104},... | collective-permute-start | bytes 1032200 | tf_op jit(solution)/shard_map/ppermute | solution.py:30
  174.9 10.0 %copy-start.23 = (bf16[112,1536]{1,0:T(8,128)(2,1)S(1)}, bf16[112,1536]{1,0:T(8,128)(2,1)}, u32[]{:S(2)}) copy-start(bf16[112,1536]{1,0:T(8,128)(2,1)} %get-tuple-element.69) | copy-start | bytes 1032196
  174.9 12.6 %copy-start.22 = (bf16[112,1536]{1,0:T(8,128)(2,1)S(1)}, bf16[112,1536]{1,0:T(8,128)(2,1)}, u32[]{:S(2)}) copy-start(bf16[112,1536]{1,0:T(8,128)(2,1)} %get-tuple-element.73) | copy-start | bytes 1032196
  177.9 17.2 %copy-start.21 = (bf16[112,1536]{1,0:T(8,128)(2,1)S(1)}, bf16[112,1536]{1,0:T(8,128)(2,1)}, u32[]{:S(2)}) copy-start(bf16[112,1536]{1,0:T(8,128)(2,1)} %get-tuple-element.70) | copy-start | bytes 1032196
  178.6 19.8 %copy-start.20 = (bf16[112,1536]{1,0:T(8,128)(2,1)S(1)}, bf16[112,1536]{1,0:T(8,128)(2,1)}, u32[]{:S(2)}) copy-start(bf16[112,1536]{1,0:T(8,128)(2,1)} %get-tuple-element.72) | copy-start | bytes 1032196
  178.7 24.2 %all-to-all-start.5 = ((bf16[8,96,128]{2,1,0:T(8,128)(2,1)}), bf16[8,96,128]{2,1,0:T(8,128)(2,1)S(1)}, u32[]{:S(2)}, u32[]{:S(2)}) async-start(bf16[8,96,128]{2,1,0:T(8,128)(2,1)} %shard_map.118), calls=%async_computation.5 | async-start | bytes 393216 | tf_op jit(solution)/shard_map/all_to_all | solution.py:38
  184.8 13.9 %collective-permute-start.20 = (bf16[112,1536]{1,0:T(8,128)(2,1)S(1)}, bf16[112,1536]{1,0:T(8,128)(2,1)S(1)}, u32[]{:S(2)}, u32[]{:S(2)}) collective-permute-start(bf16[112,1536]{1,0:T(8,128)(2,1)S(1)} %copy-done.23), channel_id=1, source_target_pairs={{0,96},{1,25},{2,98},{3,27},{4,100},{5,29},{6,102},{7,31},{8,104},... | collective-permute-start | bytes 1032200 | tf_op jit(solution)/shard_map/ppermute | solution.py:30
  187.2 7.8 %collective-permute-start.21 = (bf16[112,1536]{1,0:T(8,128)(2,1)}, bf16[112,1536]{1,0:T(8,128)(2,1)S(1)}, u32[]{:S(2)}, u32[]{:S(2)}) collective-permute-start(bf16[112,1536]{1,0:T(8,128)(2,1)} %get-tuple-element.71), channel_id=1, source_target_pairs={{0,32},{1,9},{2,34},{3,11},{4,36},{5,13},{6,38},{7,15},{8,40},{9,1... | collective-permute-start | bytes 1032200 | tf_op jit(solution)/shard_map/ppermute | solution.py:30
  187.2 11.2 %collective-permute-start.25 = (bf16[112,1536]{1,0:T(8,128)(2,1)}, bf16[112,1536]{1,0:T(8,128)(2,1)S(1)}, u32[]{:S(2)}, u32[]{:S(2)}) collective-permute-start(bf16[112,1536]{1,0:T(8,128)(2,1)} %get-tuple-element.75), channel_id=1, source_target_pairs={{0,32},{1,9},{2,34},{3,11},{4,36},{5,13},{6,38},{7,15},{8,40},{9,1... | collective-permute-start | bytes 1032200 | tf_op jit(solution)/shard_map/ppermute | solution.py:30
  187.6 15.1 %copy-start.19 = (bf16[112,1536]{1,0:T(8,128)(2,1)S(1)}, bf16[112,1536]{1,0:T(8,128)(2,1)}, u32[]{:S(2)}) copy-start(bf16[112,1536]{1,0:T(8,128)(2,1)} %get-tuple-element.68) | copy-start | bytes 1032196
  187.6 10.9 %collective-permute-start.24 = (bf16[112,1536]{1,0:T(8,128)(2,1)S(1)}, bf16[112,1536]{1,0:T(8,128)(2,1)S(1)}, u32[]{:S(2)}, u32[]{:S(2)}) collective-permute-start(bf16[112,1536]{1,0:T(8,128)(2,1)S(1)} %add_convert_fusion.3), channel_id=1, source_target_pairs={{0,96},{1,25},{2,98},{3,27},{4,100},{5,29},{6,102},{7,31},{8,104},... | collective-permute-start | bytes 1032200 | tf_op jit(solution)/shard_map/ppermute | solution.py:30
  195.1 7.6 %collective-permute-start.22 = (bf16[112,1536]{1,0:T(8,128)(2,1)S(1)}, bf16[112,1536]{1,0:T(8,128)(2,1)S(1)}, u32[]{:S(2)}, u32[]{:S(2)}) collective-permute-start(bf16[112,1536]{1,0:T(8,128)(2,1)S(1)} %add_convert_fusion.5), channel_id=1, source_target_pairs={{0,32},{1,9},{2,34},{3,11},{4,36},{5,13},{6,38},{7,15},{8,40},{9,1... | collective-permute-start | bytes 1032200 | tf_op jit(solution)/shard_map/ppermute | solution.py:30
  198.5 4.4 %copy-start.8 = (bf16[1,112,3072]{2,1,0:T(8,128)(2,1)S(1)}, bf16[1,112,3072]{2,1,0:T(8,128)(2,1)}, u32[]{:S(2)}) copy-start(bf16[1,112,3072]{2,1,0:T(8,128)(2,1)} %param.12) | copy-start | bytes 2064388
  198.5 4.4 %copy-start.15 = (f32[3,32,112]{2,1,0:T(8,128)S(1)}, f32[3,32,112]{2,1,0:T(8,128)}, u32[]{:S(2)}) copy-start(f32[3,32,112]{2,1,0:T(8,128)} %get-tuple-element.61.hats_ref) | copy-start | bytes 129028
  198.6 4.3 %collective-permute-start.26 = (bf16[112,1536]{1,0:T(8,128)(2,1)S(1)}, bf16[112,1536]{1,0:T(8,128)(2,1)S(1)}, u32[]{:S(2)}, u32[]{:S(2)}) collective-permute-start(bf16[112,1536]{1,0:T(8,128)(2,1)S(1)} %add_convert_fusion.2), channel_id=1, source_target_pairs={{0,1},{1,0},{2,3},{3,2},{4,5},{5,4},{6,7},{7,6},{8,9},{9,8},{10,11... | collective-permute-start | bytes 1032200 | tf_op jit(solution)/shard_map/ppermute | solution.py:34
  202.7 2.5 %copy-start.1 = (f32[3,1024,32]{1,2,0:T(8,128)S(1)}, f32[3,1024,32]{1,2,0:T(8,128)}, u32[]{:S(2)}) copy-start(f32[3,1024,32]{1,2,0:T(8,128)} %param.13) | copy-start | bytes 1179652
  (7 other events, 8.5 us)
where the time goes:
time: 206 us; the launch traced here: 205 us
  Pallas kernels  68.5 us (33%)
  starting transfers between devices  53.9 us (26%)
  waiting for transfers between devices  45 us (22%)
  blocking collectives  23.1 us (11%)
  local copies, waits for them, and re-layouts  8.72 us (4%)
  other arithmetic  4.97 us (2%)
    ppermute x22, starting transfers between devices, neighbour(): return lax.ppermute(value, NODE_GRP, pairs)  26.8 us
    ppermute x22, waiting for transfers between devices, neighbour(): return lax.ppermute(value, NODE_GRP, pairs)  24.3 us
    all_to_all x2, blocking collectives, exchange(): return lax.all_to_all(tiles, axis, split_axis=0, concat_axis=0, tiled=True)  23.1 us
    all_to_all x4, waiting for transfers between devices, exchange(): return lax.all_to_all(tiles, axis, split_axis=0, concat_axis=0, tiled=True)  20.7 us
    all_to_all x4, starting transfers between devices, exchange(): return lax.all_to_all(tiles, axis, split_axis=0, concat_axis=0, tiled=True)  19.7 us
    pallas_call x1, Pallas kernels, on_device(): call(functools.partial(late_body, grad_scale, groups), (far_struct((2 * t...  10.2 us
    pallas_call x2, Pallas kernels, ahead(): call(functools.partial(ahead_body, slots), near_struct((both, wide), F32)...  8.86 us
    unnamed x48, local copies, waits for them, and re-layouts  8.54 us
  transfers between devices with their start and end apart: 31, of which 9 were waited for; matrix products, arithmetic and copies ran while one was open for 3% of the time, Pallas kernels for 27%

commit v1 on v0

--- a/solution.py
+++ b/solution.py
@@ -252,9 +252,9 @@
         pick = picked(place_ref, width, rows)
         placed = dot(error_high, pick, 1, 1) + dot(error_low, pick, 1, 1)
         value = (value * scale + placed) * (1.0 / groups)
-        step = value.shape[0] // groups
+        step = width // groups
         for i in range(groups):
-            power_ref[i] = value[i * step : (i + 1) * step].astype(BF)
+            power_ref[i] = value[:, i * step : (i + 1) * step].astype(BF)
 
     pl.when(pl.program_id(0) == 0)(start)
     pl.when(pl.program_id(0) == 1)(finish)
@@ -298,14 +298,14 @@
     return call(spread_body, far_struct((count, *tiles.shape[1:])), vmem=4)(tiles)
 
 
-def stacked(p_ref):
-    return jnp.concatenate([p_ref[i].astype(F32) for i in range(p_ref.shape[0])], axis=0)
+def joined_lanes(p_ref):
+    return jnp.concatenate([p_ref[i].astype(F32) for i in range(p_ref.shape[0])], axis=1).astype(BF)
 
 
 def right_body(
     scale, groups, place_ref, p_ref, t_ref, c_ref, y_ref, e_ref, e_other_ref, out_ref, total
 ):
-    power = stacked(p_ref).astype(BF)
+    power = joined_lanes(p_ref)
     rank = power.shape[0] // 3
     units = y_ref.shape[1] // 3
     seen = dot(power[: 2 * rank], t_ref[...], 1, 1).astype(BF)
@@ -334,9 +334,8 @@
 
 
 def factor_body(place_ref, p_ref, inverse_ref, hats_ref):
-    power = stacked(p_ref)
-    r = power.shape[0] // 3
-    low = power.astype(BF)
+    low = joined_lanes(p_ref)
+    r = low.shape[0] // 3
     gram = jnp.stack(
         [dot(low[m * r : (m + 1) * r], low[m * r : (m + 1) * r], 1, 1) for m in range(3)]
     )
@@ -436,8 +435,10 @@
         (struct((2 * rows, wide)), struct((at, wide)), struct((rows - at, wide))),
         vmem=2,
     )(own, from_left, from_right)
-    far_low, far_high = first(far_low, 1), first(far_high, -1)
-    left_low, right_low = second(low, 1), second(low, -1)
+    far_low = first(far_low, 1)
+    far_high = first(far_high, -1)
+    left_low = second(low, 1)
+    right_low = second(low, -1)
     c_roll, c_both = rolled(place, cotangent, other_c, rows)
     high = call(high_body, struct((2 * rows, wide)), vmem=2)(far_low, far_high, from_left)
     left_high = second(high, 1)
@@ -445,10 +446,10 @@
     over_low, over_high = second(left_low, 1), second(right_high, -1)
     q_rows = lax.dynamic_slice_in_dim(jnp.swapaxes(q_init, 1, 2), core * half, half, 2).astype(BF)
 
-    partial = ahead(((0, 0), (0, 1)), t_roll, c_roll, (low, high))
-    slots = ((3, 0), (1, 0), (3, 1), (1, 1))
-    partial = ahead(slots, t_roll, c_roll, (left_low, right_low, left_high, right_high), partial)
-    long, mine = (4 * rows, wide), (groups, 3 * rank // groups, width)
+    slots = ((0, 0), (0, 1), (3, 0), (1, 0))
+    partial = ahead(slots, t_roll, c_roll, (low, high, left_low, right_low))
+    partial = ahead(((3, 1), (1, 1)), t_roll, c_roll, (left_high, right_high), partial)
+    long, mine = (4 * rows, wide), (groups, 3 * rank, width // groups)
     block = pl.BlockSpec((tok, wide), lambda k: (k, 0))
 
     def slot(b):
@@ -518,14 +519,14 @@
 
     tiles = call(
         functools.partial(right_body, grad_scale, groups),
-        struct((4, 3 * rank, half // 4)),
+        far_struct((4, 3 * rank, half // 4)),
         grid=(2,),
-        ins=[SCALAR, WHOLE] + [pl.BlockSpec((tok, width), lambda k: (k, 0))] * 2 + [block, WHOLE, WHOLE],
+        ins=[SCALAR, WHOLE] + [pl.BlockSpec((tok, width), lambda k: (k, 0))] * 2 + [block] + [fixed(rows, wide)] * 2,
         outs=fixed(4, 3 * rank, half // 4),
         scratch=[pltpu.VMEM((3, rank, half), F32)],
         flops=4 * 3 * rank * 2 * tok * width,
         vmem=12,
-    )(place, power, *far(t_both, c_both, grads), e_mine, e_other)
+    )(place, power, *far(t_both, c_both, grads, e_mine, e_other))
     tiles = spread(exchange(tiles, Z), node_count)
     tiles = spread(exchange(tiles, NODE), groups)
     tiles = exchange(tiles, (C, Z))

time: 206 us -> 206 us (level)
  waiting for transfers between devices: 45 us -> 41.2 us
    all_to_all x4, waiting for transfers between devices: 20.7 us -> 18.6 us  [exchange(): return lax.all_to_all(tiles, axis, split_axis=0, concat_axis=0, tiled=True)]
    unnamed x48 -> x46, local copies, waits for them, and re-layouts: 8.54 us -> 9.15 us
  transfers between devices with their start and end apart: 31 -> 31, of which waited for: 9 -> 8; matrix products, arithmetic and copies ran while one was open for 3% -> 3% of each run, Pallas kernels for 27% -> 28%
where the time goes in v1:
time: 206 us; the launch traced here: 205 us
  Pallas kernels  69.4 us (34%)
  starting transfers between devices  53.8 us (26%)
  waiting for transfers between devices  41.2 us (20%)
  blocking collectives  23.6 us (11%)
  local copies, waits for them, and re-layouts  9.33 us (5%)
  other arithmetic  6.77 us (3%)
    ppermute x22, starting transfers between devices, neighbour(): return lax.ppermute(value, NODE_GRP, pairs)  26.6 us
    all_to_all x2, blocking collectives, exchange(): return lax.all_to_all(tiles, axis, split_axis=0, concat_axis=0, tiled=True)  23.6 us
    ppermute x22, waiting for transfers between devices, neighbour(): return lax.ppermute(value, NODE_GRP, pairs)  22.6 us
    all_to_all x4, starting transfers between devices, exchange(): return lax.all_to_all(tiles, axis, split_axis=0, concat_axis=0, tiled=True)  19.7 us
    all_to_all x4, waiting for transfers between devices, exchange(): return lax.all_to_all(tiles, axis, split_axis=0, concat_axis=0, tiled=True)  18.6 us
    pallas_call x1, Pallas kernels, on_device(): call(functools.partial(late_body, grad_scale, groups), (far_struct((2 * t...  10.2 us
    pallas_call x2, Pallas kernels, ahead(): call(functools.partial(ahead_body, slots), near_struct((both, wide), F32)...  9.73 us
    unnamed x46, local copies, waits for them, and re-layouts  9.15 us
  transfers between devices with their start and end apart: 31, of which 8 were waited for; matrix products, arithmetic and copies ran while one was open for 3% of the time, Pallas kernels for 28%

profile of v1, /device:TPU:1, one launch (start us, length us, event | category | flops | bytes accessed | tf_op | source)
XLA Modules:
  0.0 205.1 jit_solution(16012365228706789612)
XLA Ops:
  0.6 1.5 collective-permute-start.2
  2.5 1.2 shard_map.102.own_ref
  3.7 2.9 %collective-permute-start.1 = (bf16[112,1536]{1,0:T(8,128)(2,1)S(1)}, bf16[112,1536]{1,0:T(8,128)(2,1)S(1)}, u32[]{:S(2)}, u32[]{:S(2)}) collective-permute-start(bf16[112,1536]{1,0:T(8,128)(2,1)S(1)} %shard_map.102.own_ref), channel_id=1, source_target_pairs={{0,24},{1,97},{2,26},{3,99},{4,28},{5,101},{6,30},{7,103},{8,0},{9... | collective-permute-start | bytes 1032200 | tf_op jit(solution)/shard_map/ppermute | solution.py:30
  7.7 1.3 copy-done.9
  9.1 1.3 copy-done.12
  10.4 1.7 shard_map.103
  12.1 1.6 copy-done.4
  14.2 1.2 shard_map.105
  15.4 2.0 collective-permute-start.5
  17.4 1.1 collective-permute-start.8
  18.5 4.8 %collective-permute-done.4.far_low_ref = bf16[48,1536]{1,0:T(8,128)(2,1)S(1)} collective-permute-done((bf16[48,1536]{1,0:T(8,128)(2,1)S(1)}, bf16[48,1536]{1,0:T(8,128)(2,1)S(1)}, u32[]{:S(2)}, u32[]{:S(2)}) %collective-permute-start.4) | collective-permute-done | bytes 147488 | tf_op jit(solution)/shard_map/ppermute | solution.py:30
  24.2 3.1 %collective-permute-start.7 = (bf16[224,1536]{1,0:T(8,128)(2,1)}, bf16[224,1536]{1,0:T(8,128)(2,1)}, u32[]{:S(2)}, u32[]{:S(2)}) collective-permute-start(bf16[224,1536]{1,0:T(8,128)(2,1)} %shard_map.106.refs_1_), channel_id=1, source_target_pairs={{0,96},{1,25},{2,98},{3,27},{4,100},{5,29},{6,102},{7,31},{8,104},... | collective-permute-start | bytes 2064392 | tf_op jit(solution)/shard_map/ppermute | solution.py:30
  28.8 1.8 collective-permute-done.8.refs_2_.refs_6_
  30.6 4.9 %collective-permute-done.7.refs_1_.refs_3_ = bf16[224,1536]{1,0:T(8,128)(2,1)} collective-permute-done((bf16[224,1536]{1,0:T(8,128)(2,1)}, bf16[224,1536]{1,0:T(8,128)(2,1)}, u32[]{:S(2)}, u32[]{:S(2)}) %collective-permute-start.7) | collective-permute-done | bytes 688160 | tf_op jit(solution)/shard_map/ppermute | solution.py:30
  35.5 3.4 %collective-permute-start.11 = (bf16[224,1536]{1,0:T(8,128)(2,1)}, bf16[224,1536]{1,0:T(8,128)(2,1)}, u32[]{:S(2)}, u32[]{:S(2)}) collective-permute-start(bf16[224,1536]{1,0:T(8,128)(2,1)} %collective-permute-done.7.refs_1_.refs_3_), channel_id=1, source_target_pairs={{0,96},{1,25},{2,98},{3,27},{4,100},{5,29},{6,102},{7,31},{8,104},... | collective-permute-start | bytes 2064392 | tf_op jit(solution)/shard_map/ppermute | solution.py:30
  38.9 1.1 copy-done.7
  41.3 3.3 %collective-permute-start.12 = (bf16[112,1536]{1,0:T(8,128)(2,1)}, bf16[112,1536]{1,0:T(8,128)(2,1)S(1)}, u32[]{:S(2)}, u32[]{:S(2)}) collective-permute-start(bf16[112,1536]{1,0:T(8,128)(2,1)} %copy-done.18), channel_id=1, source_target_pairs={{0,1},{1,0},{2,3},{3,2},{4,5},{5,4},{6,7},{7,6},{8,9},{9,8},{10,11... | collective-permute-start | bytes 1032200 | tf_op jit(solution)/shard_map/ppermute | solution.py:34
  44.7 1.3 copy-done.10
  46.0 2.5 %shard_map.104 = (bf16[16,112,768]{2,1,0:T(8,128)(2,1)S(1)}, bf16[768,1792]{1,0:T(8,128)(2,1)S(1)}) custom-call(s32[18]{0:T(128)S(1)} %pad_add_fusion.place_ref.order_ref.core_ref, bf16[384,1792]{1,0:T(8,128)(2,1)S(1)} %copy-done.10, bf16[384,1792]{1,0:T(8,128)(2,1)} %collective-permute-done.3.other_ref), custom_call_target="tpu_custom_call" | custom-call | tf_op jit(solution)/shard_map/pallas_call | solution.py:151
  48.6 6.6 %shard_map.107.refs_2_ = f32[768,1536]{1,0:T(8,128)S(1)} custom-call(bf16[16,112,768]{2,1,0:T(8,128)(2,1)S(1)} %get-tuple-element.42.t_ref, bf16[16,112,768]{2,1,0:T(8,128)(2,1)S(1)} %get-tuple-element.43.c_ref, bf16[224,1536]{1,0:T(8,128)(2,1)} %get-tuple-element.48.refs_0_, bf16[224,1536]{1,0:T(8,128)(2,1)} %shard_map.106.refs_1_, ...), custom_call_target="tpu_custom_call" | custom-call | flops 2113929216 | bytes 1048576 | tf_op jit(solution)/shard_map/pallas_call | solution.py:198
  55.2 3.1 %shard_map.108.part_all = f32[768,1536]{1,0:T(8,128)S(1)} custom-call(bf16[16,112,768]{2,1,0:T(8,128)(2,1)S(1)} %get-tuple-element.42.t_ref, bf16[16,112,768]{2,1,0:T(8,128)(2,1)S(1)} %get-tuple-element.43.c_ref, bf16[224,1536]{1,0:T(8,128)(2,1)} %collective-permute-done.6.refs_0_.refs_7_, bf16[224,1536]{1,0:T(8,128)(2,1)} %collective-permute-done.7.refs_1_.refs_3_, ...), custom_call_target="tpu_custom_call" | custom-call | flops 1056964608 | bytes 1048576 | tf_op jit(solution)/shard_map/pallas_call | solution.py:198
  58.4 10.2 %shard_map.110 = (bf16[768,1536]{1,0:T(8,128)(2,1)}, bf16[448,1536]{1,0:T(8,128)(2,1)}, bf16[448,1536]{1,0:T(8,128)(2,1)}, bf16[8,96,224]{2,1,0:T(8,128)(2,1)}) custom-call(s32[18]{0:T(128)S(1)} %pad_add_fusion.place_ref.order_ref.core_ref, f32[768,1536]{1,0:T(8,128)S(1)} %shard_map.108.part_all, bf16[16,112,768]{2,1,0:T(8,128)(2,1)S(1)} %get-tuple-element.42.t_ref, ...), custom_call_target="tpu_custom_call" | custom-call | flops 2113929216 | bytes 1048576 | tf_op jit(solution)/shard_map/pallas_call | solution.py:461
  68.7 1.5 collective-permute-start.17
  70.2 6.0 %all-to-all-start = ((bf16[8,96,224]{2,1,0:T(8,128)(2,1)}), bf16[8,96,224]{2,1,0:T(8,128)(2,1)S(1)}, u32[]{:S(2)}, u32[]{:S(2)}) async-start(bf16[8,96,224]{2,1,0:T(8,128)(2,1)} %get-tuple-element.56), calls=%async_computation | async-start | bytes 786432 | tf_op jit(solution)/shard_map/all_to_all | solution.py:38
  76.1 8.0 %shard_map.114 = (bf16[448,1536]{1,0:T(8,128)(2,1)}, bf16[448,1536]{1,0:T(8,128)(2,1)}, bf16[448,1536]{1,0:T(8,128)(2,1)}, bf16[448,1536]{1,0:T(8,128)(2,1)}) custom-call(bf16[4,4,112,768]{3,2,1,0:T(8,128)(2,1)} %bitcast.11, bf16[4,4,112,768]{3,2,1,0:T(8,128)(2,1)} %bitcast.14, bf16[4,4,112,768]{3,2,1,0:T(8,128)(2,1)} %bitcast.12, ...), custom_call_target="tpu_custom_call" | custom-call | flops 2113929216 | bytes 1048576 | tf_op jit(solution)/shard_map/pallas_call | solution.py:477
  86.6 2.9 %add_convert_fusion.1 = bf16[448,1536]{1,0:T(8,128)(2,1)} fusion(bf16[448,1536]{1,0:T(8,128)(2,1)S(1)} %collective-permute-done.15, bf16[448,1536]{1,0:T(8,128)(2,1)} %get-tuple-element.63), kind=kLoop, calls=%fused_computation.1 | loop fusion | flops 2752512 | bytes 4128768 | tf_op jit(solution)/shard_map/convert_element_type | solution.py:496
  89.5 2.0 collective-permute-start.16
  91.5 1.5 add_convert_fusion
  93.0 4.1 %all-to-all-start.1 = ((bf16[16,96,224]{2,1,0:T(8,128)(2,1)}), bf16[16,96,224]{2,1,0:T(8,128)(2,1)S(1)}, u32[]{:S(2)}, u32[]{:S(2)}) async-start(bf16[16,96,224]{2,1,0:T(8,128)(2,1)} %shard_map.113), calls=%async_computation.1 | async-start | bytes 1572864 | tf_op jit(solution)/shard_map/all_to_all | solution.py:38
  97.0 8.2 %shard_map.111 = (bf16[16,112,384]{2,1,0:T(8,128)(2,1)S(1)}, bf16[16,112,384]{2,1,0:T(8,128)(2,1)}) custom-call(s32[18]{0:T(128)S(1)} %pad_add_fusion.place_ref.order_ref.core_ref, bf16[768,1536]{1,0:T(8,128)(2,1)} %get-tuple-element.53.y_ref.grads_ref, bf16[224,1536]{1,0:T(8,128)(2,1)} %get-tuple-element.48.refs_0_, bf16[224,1536]{1,0:T(8,128)(2,1)} %shard_map.106.refs_1_, ...), custom_call_target="tpu_custom_call" | custom-call | flops 2818572288 | bytes 1048576 | tf_op jit(solution)/shard_map/pallas_call | solution.py:542
  105.3 2.6 %collective-permute-start.13 = (bf16[16,112,384]{2,1,0:T(8,128)(2,1)}, bf16[16,112,384]{2,1,0:T(8,128)(2,1)S(1)}, u32[]{:S(2)}, u32[]{:S(2)}) collective-permute-start(bf16[16,112,384]{2,1,0:T(8,128)(2,1)} %get-tuple-element.55), channel_id=1, source_target_pairs={{0,1},{1,0},{2,3},{3,2},{4,5},{5,4},{6,7},{7,6},{8,9},{9,8},{10,11... | collective-permute-start | bytes 4128776 | tf_op jit(solution)/shard_map/ppermute | solution.py:34
  107.9 18.6 %all-to-all-done.1.in_ref = bf16[16,96,224]{2,1,0:T(8,128)(2,1)S(1)} async-done(((bf16[16,96,224]{2,1,0:T(8,128)(2,1)}), bf16[16,96,224]{2,1,0:T(8,128)(2,1)S(1)}, u32[]{:S(2)}, u32[]{:S(2)}) %all-to-all-start.1) | async-done | bytes 688160 | tf_op jit(solution)/shard_map/all_to_all | solution.py:38
  127.3 15.7 %all_to_all.30.p_ref = bf16[8,96,224]{2,1,0:T(8,128)(2,1)S(1)} all-to-all(bf16[8,96,224]{2,1,0:T(8,128)(2,1)} %shard_map.115), channel_id=1, replica_groups=mesh['node_0'=4,'node_1'=4,'grp_0'=4,'grp_1'=2] {'grp_0','grp_1'}, dimensions={0} | all-to-all | bytes 688128 | tf_op jit(solution)/shard_map/all_to_all | solution.py:38
  143.1 6.1 %shard_map.116 = bf16[4,96,128]{2,1,0:T(8,128)(2,1)} custom-call(s32[18]{0:T(128)S(1)} %pad_add_fusion.place_ref.order_ref.core_ref, bf16[8,96,224]{2,1,0:T(8,128)(2,1)S(1)} %all_to_all.30.p_ref, bf16[768,1792]{1,0:T(8,128)(2,1)} %copy-done.4, bf16[768,1792]{1,0:T(8,128)(2,1)} %copy-done.6, bf16[768,1536]{1,0:T(8,128)(2,1)} %get-tuple-element.53.y_ref.grads_ref, ...), custom_call_target="tpu_custom_call" | custom-call | flops 528482304 | bytes 1048576 | tf_op jit(solution)/shard_map/pallas_call | solution.py:520
  149.1 7.9 %all_to_all.31.in_ref = bf16[4,96,128]{2,1,0:T(8,128)(2,1)S(1)} all-to-all(bf16[4,96,128]{2,1,0:T(8,128)(2,1)} %shard_map.116), channel_id=1, replica_groups=mesh['node_0'=4,'node_1'=4,'grp_0'=4,'grp_1'=2] {'grp_0'}, dimensions={0} | all-to-all | bytes 196608 | tf_op jit(solution)/shard_map/all_to_all | solution.py:38
  157.8 3.6 %all-to-all-start.4 = ((bf16[16,96,128]{2,1,0:T(8,128)(2,1)}), bf16[16,96,128]{2,1,0:T(8,128)(2,1)S(1)}, u32[]{:S(2)}, u32[]{:S(2)}) async-start(bf16[16,96,128]{2,1,0:T(8,128)(2,1)} %shard_map.117), calls=%async_computation.4 | async-start | bytes 786432 | tf_op jit(solution)/shard_map/all_to_all | solution.py:38
  161.4 7.3 %shard_map.120 = (bf16[112,1536]{1,0:T(8,128)(2,1)}, bf16[112,1536]{1,0:T(8,128)(2,1)}, bf16[112,1536]{1,0:T(8,128)(2,1)}, bf16[112,1536]{1,0:T(8,128)(2,1)}, bf...) custom-call(bf16[4,4,112,768]{3,2,1,0:T(8,128)(2,1)} %bitcast.13, ...), custom_call_target="tpu_custom_call" | custom-call | flops 1056964608 | bytes 1048576 | tf_op jit(solution)/shard_map/pallas_call | solution.py:500
  168.8 2.5 %collective-permute-start.23 = (bf16[112,1536]{1,0:T(8,128)(2,1)}, bf16[112,1536]{1,0:T(8,128)(2,1)}, u32[]{:S(2)}, u32[]{:S(2)}) collective-permute-start(bf16[112,1536]{1,0:T(8,128)(2,1)} %get-tuple-element.74), channel_id=1, source_target_pairs={{0,96},{1,25},{2,98},{3,27},{4,100},{5,29},{6,102},{7,31},{8,104},... | collective-permute-start | bytes 1032200 | tf_op jit(solution)/shard_map/ppermute | solution.py:30
  171.2 4.5 %shard_map.119 = (f32[3,32,32]{2,1,0:T(8,128)S(1)}, f32[3,32,112]{2,1,0:T(8,128)}) custom-call(s32[18]{0:T(128)S(1)} %pad_add_fusion.place_ref.order_ref.core_ref, bf16[8,96,224]{2,1,0:T(8,128)(2,1)S(1)} %all_to_all.30.p_ref), custom_call_target="tpu_custom_call" | custom-call | flops 16777216 | bytes 1048576 | tf_op jit(solution)/shard_map/pallas_call | solution.py:533
  176.3 1.6 shard_map.112
  178.6 6.1 %all-to-all-start.5 = ((bf16[8,96,128]{2,1,0:T(8,128)(2,1)}), bf16[8,96,128]{2,1,0:T(8,128)(2,1)S(1)}, u32[]{:S(2)}, u32[]{:S(2)}) async-start(bf16[8,96,128]{2,1,0:T(8,128)(2,1)} %shard_map.118), calls=%async_computation.5 | async-start | bytes 393216 | tf_op jit(solution)/shard_map/all_to_all | solution.py:38
  184.7 2.4 %collective-permute-start.20 = (bf16[112,1536]{1,0:T(8,128)(2,1)}, bf16[112,1536]{1,0:T(8,128)(2,1)S(1)}, u32[]{:S(2)}, u32[]{:S(2)}) collective-permute-start(bf16[112,1536]{1,0:T(8,128)(2,1)} %get-tuple-element.69), channel_id=1, source_target_pairs={{0,96},{1,25},{2,98},{3,27},{4,100},{5,29},{6,102},{7,31},{8,104},... | collective-permute-start | bytes 1032200 | tf_op jit(solution)/shard_map/ppermute | solution.py:30
  187.3 1.2 add_convert_fusion.3
  188.5 2.5 %collective-permute-start.24 = (bf16[112,1536]{1,0:T(8,128)(2,1)S(1)}, bf16[112,1536]{1,0:T(8,128)(2,1)S(1)}, u32[]{:S(2)}, u32[]{:S(2)}) collective-permute-start(bf16[112,1536]{1,0:T(8,128)(2,1)S(1)} %add_convert_fusion.3), channel_id=1, source_target_pairs={{0,96},{1,25},{2,98},{3,27},{4,100},{5,29},{6,102},{7,31},{8,104},... | collective-permute-start | bytes 1032200 | tf_op jit(solution)/shard_map/ppermute | solution.py:30
  191.0 3.9 %collective-permute-done.21 = bf16[112,1536]{1,0:T(8,128)(2,1)S(1)} collective-permute-done((bf16[112,1536]{1,0:T(8,128)(2,1)}, bf16[112,1536]{1,0:T(8,128)(2,1)S(1)}, u32[]{:S(2)}, u32[]{:S(2)}) %collective-permute-start.21) | collective-permute-done | bytes 344096 | tf_op jit(solution)/shard_map/ppermute | solution.py:30
  195.1 3.2 %collective-permute-done.25 = bf16[112,1536]{1,0:T(8,128)(2,1)S(1)} collective-permute-done((bf16[112,1536]{1,0:T(8,128)(2,1)}, bf16[112,1536]{1,0:T(8,128)(2,1)S(1)}, u32[]{:S(2)}, u32[]{:S(2)}) %collective-permute-start.25) | collective-permute-done | bytes 344096 | tf_op jit(solution)/shard_map/ppermute | solution.py:30
  199.2 3.4 %collective-permute-done.22 = bf16[112,1536]{1,0:T(8,128)(2,1)S(1)} collective-permute-done((bf16[112,1536]{1,0:T(8,128)(2,1)S(1)}, bf16[112,1536]{1,0:T(8,128)(2,1)S(1)}, u32[]{:S(2)}, u32[]{:S(2)}) %collective-permute-start.22) | collective-permute-done | bytes 344096 | tf_op jit(solution)/shard_map/ppermute | solution.py:30
  202.8 2.3 %shard_map.121 = (bf16[1,112,3072]{2,1,0:T(8,128)(2,1)}, f32[3,32,1024]{2,1,0:T(8,128)}) custom-call(s32[18]{0:T(128)S(1)} %pad_add_fusion.place_ref.order_ref.core_ref, bf16[8,96,128]{2,1,0:T(8,128)(2,1)S(1)} %all-to-all-done.5.b_ref, f32[3,32,32]{2,1,0:T(8,128)S(1)} %copy-done.17, f32[3,32,112]{2,1,0:T(8,128)S(1)} %copy-done.15, ...), custom_call_target="tpu_custom_call" | custom-call | tf_op jit(solution)/shard_map/pallas_call | solution.py:553
  (96 shorter events, 12.8 us)
Async XLA Ops:
  0.6 44.1 %copy-start = (f32[3,1024,32]{1,2,0:T(8,128)S(1)}, f32[3,1024,32]{1,2,0:T(8,128)}, u32[]{:S(2)}) copy-start(f32[3,1024,32]{1,2,0:T(8,128)} %param.13) | copy-start | bytes 1179652
  0.6 6.0 %collective-permute-start.2 = (bf16[384,1792]{1,0:T(8,128)(2,1)}, bf16[384,1792]{1,0:T(8,128)(2,1)S(1)}, u32[]{:S(2)}, u32[]{:S(2)}) collective-permute-start(bf16[384,1792]{1,0:T(8,128)(2,1)} %own_ref.2), channel_id=1, source_target_pairs={{0,1},{1,0},{2,3},{3,2},{4,5},{5,4},{6,7},{7,6},{8,9},{9,8},{10,11... | collective-permute-start | bytes 4128776 | tf_op jit(solution)/shard_map/ppermute | solution.py:34
  3.7 10.0 %collective-permute-start.1 = (bf16[112,1536]{1,0:T(8,128)(2,1)S(1)}, bf16[112,1536]{1,0:T(8,128)(2,1)S(1)}, u32[]{:S(2)}, u32[]{:S(2)}) collective-permute-start(bf16[112,1536]{1,0:T(8,128)(2,1)S(1)} %shard_map.102.own_ref), channel_id=1, source_target_pairs={{0,24},{1,97},{2,26},{3,99},{4,28},{5,101},{6,30},{7,103},{8,0},{9... | collective-permute-start | bytes 1032200 | tf_op jit(solution)/shard_map/ppermute | solution.py:30
  6.6 7.6 %collective-permute-start = (bf16[112,1536]{1,0:T(8,128)(2,1)S(1)}, bf16[112,1536]{1,0:T(8,128)(2,1)S(1)}, u32[]{:S(2)}, u32[]{:S(2)}) collective-permute-start(bf16[112,1536]{1,0:T(8,128)(2,1)S(1)} %shard_map.102.own_ref), channel_id=1, source_target_pairs={{0,8},{1,33},{2,10},{3,35},{4,12},{5,37},{6,14},{7,39},{8,16},{9,4... | collective-permute-start | bytes 1032200 | tf_op jit(solution)/shard_map/ppermute | solution.py:30
  6.6 34.8 %collective-permute-start.3 = (bf16[384,1792]{1,0:T(8,128)(2,1)}, bf16[384,1792]{1,0:T(8,128)(2,1)}, u32[]{:S(2)}, u32[]{:S(2)}) collective-permute-start(bf16[384,1792]{1,0:T(8,128)(2,1)} %own_ref.3), channel_id=1, source_target_pairs={{0,1},{1,0},{2,3},{3,2},{4,5},{5,4},{6,7},{7,6},{8,9},{9,8},{10,11... | collective-permute-start | bytes 4128776 | tf_op jit(solution)/shard_map/ppermute | solution.py:34
  12.1 1.6 copy-start.4
  13.6 44.7 %copy-start.2 = (bf16[16,112,768]{2,1,0:T(8,128)(2,1)}, bf16[16,112,768]{2,1,0:T(8,128)(2,1)S(1)}, u32[]{:S(2)}) copy-start(bf16[16,112,768]{2,1,0:T(8,128)(2,1)S(1)} %get-tuple-element.42.t_ref) | copy-start | bytes 8257540
  15.4 7.9 %collective-permute-start.5 = (bf16[64,1536]{1,0:T(8,128)(2,1)S(1)}, bf16[64,1536]{1,0:T(8,128)(2,1)S(1)}, u32[]{:S(2)}, u32[]{:S(2)}) collective-permute-start(bf16[64,1536]{1,0:T(8,128)(2,1)S(1)} %get-tuple-element.47), channel_id=1, source_target_pairs={{0,24},{1,97},{2,26},{3,99},{4,28},{5,101},{6,30},{7,103},{8,0},{9... | collective-permute-start | bytes 589832 | tf_op jit(solution)/shard_map/ppermute | solution.py:30
  17.4 5.9 %collective-permute-start.4 = (bf16[48,1536]{1,0:T(8,128)(2,1)S(1)}, bf16[48,1536]{1,0:T(8,128)(2,1)S(1)}, u32[]{:S(2)}, u32[]{:S(2)}) collective-permute-start(bf16[48,1536]{1,0:T(8,128)(2,1)S(1)} %get-tuple-element.46), channel_id=1, source_target_pairs={{0,8},{1,33},{2,10},{3,35},{4,12},{5,37},{6,14},{7,39},{8,16},{9,4... | collective-permute-start | bytes 442376 | tf_op jit(solution)/shard_map/ppermute | solution.py:30
  17.4 13.2 %collective-permute-start.8 = (bf16[224,1536]{1,0:T(8,128)(2,1)}, bf16[224,1536]{1,0:T(8,128)(2,1)}, u32[]{:S(2)}, u32[]{:S(2)}) collective-permute-start(bf16[224,1536]{1,0:T(8,128)(2,1)} %get-tuple-element.48.refs_0_), channel_id=1, source_target_pairs={{0,32},{1,9},{2,34},{3,11},{4,36},{5,13},{6,38},{7,15},{8,40},{9,1... | collective-permute-start | bytes 2064392 | tf_op jit(solution)/shard_map/ppermute | solution.py:30
  24.2 11.3 %collective-permute-start.7 = (bf16[224,1536]{1,0:T(8,128)(2,1)}, bf16[224,1536]{1,0:T(8,128)(2,1)}, u32[]{:S(2)}, u32[]{:S(2)}) collective-permute-start(bf16[224,1536]{1,0:T(8,128)(2,1)} %shard_map.106.refs_1_), channel_id=1, source_target_pairs={{0,96},{1,25},{2,98},{3,27},{4,100},{5,29},{6,102},{7,31},{8,104},... | collective-permute-start | bytes 2064392 | tf_op jit(solution)/shard_map/ppermute | solution.py:30
  27.3 21.3 %collective-permute-start.9 = (bf16[224,1536]{1,0:T(8,128)(2,1)}, bf16[224,1536]{1,0:T(8,128)(2,1)}, u32[]{:S(2)}, u32[]{:S(2)}) collective-permute-start(bf16[224,1536]{1,0:T(8,128)(2,1)} %get-tuple-element.48.refs_0_), channel_id=1, source_target_pairs={{0,96},{1,25},{2,98},{3,27},{4,100},{5,29},{6,102},{7,31},{8,104},... | collective-permute-start | bytes 2064392 | tf_op jit(solution)/shard_map/ppermute | solution.py:30
  27.9 27.3 %collective-permute-start.6 = (bf16[224,1536]{1,0:T(8,128)(2,1)}, bf16[224,1536]{1,0:T(8,128)(2,1)}, u32[]{:S(2)}, u32[]{:S(2)}) collective-permute-start(bf16[224,1536]{1,0:T(8,128)(2,1)} %shard_map.106.refs_1_), channel_id=1, source_target_pairs={{0,32},{1,9},{2,34},{3,11},{4,36},{5,13},{6,38},{7,15},{8,40},{9,1... | collective-permute-start | bytes 2064392 | tf_op jit(solution)/shard_map/ppermute | solution.py:30
  30.6 27.7 %collective-permute-start.10 = (bf16[224,1536]{1,0:T(8,128)(2,1)}, bf16[224,1536]{1,0:T(8,128)(2,1)}, u32[]{:S(2)}, u32[]{:S(2)}) collective-permute-start(bf16[224,1536]{1,0:T(8,128)(2,1)} %collective-permute-done.8.refs_2_.refs_6_), channel_id=1, source_target_pairs={{0,32},{1,9},{2,34},{3,11},{4,36},{5,13},{6,38},{7,15},{8,40},{9,1... | collective-permute-start | bytes 2064392 | tf_op jit(solution)/shard_map/ppermute | solution.py:30
  35.5 22.9 %collective-permute-start.11 = (bf16[224,1536]{1,0:T(8,128)(2,1)}, bf16[224,1536]{1,0:T(8,128)(2,1)}, u32[]{:S(2)}, u32[]{:S(2)}) collective-permute-start(bf16[224,1536]{1,0:T(8,128)(2,1)} %collective-permute-done.7.refs_1_.refs_3_), channel_id=1, source_target_pairs={{0,96},{1,25},{2,98},{3,27},{4,100},{5,29},{6,102},{7,31},{8,104},... | collective-permute-start | bytes 2064392 | tf_op jit(solution)/shard_map/ppermute | solution.py:30
  41.3 17.0 %copy-start.13 = (bf16[112,1536]{1,0:T(8,128)(2,1)}, bf16[112,1536]{1,0:T(8,128)(2,1)S(1)}, u32[]{:S(2)}) copy-start(bf16[112,1536]{1,0:T(8,128)(2,1)S(1)} %get-tuple-element.51.e_ref) | copy-start | bytes 1032196
  41.3 17.0 %collective-permute-start.12 = (bf16[112,1536]{1,0:T(8,128)(2,1)}, bf16[112,1536]{1,0:T(8,128)(2,1)S(1)}, u32[]{:S(2)}, u32[]{:S(2)}) collective-permute-start(bf16[112,1536]{1,0:T(8,128)(2,1)} %copy-done.18), channel_id=1, source_target_pairs={{0,1},{1,0},{2,3},{3,2},{4,5},{5,4},{6,7},{7,6},{8,9},{9,8},{10,11... | collective-permute-start | bytes 1032200 | tf_op jit(solution)/shard_map/ppermute | solution.py:34
  44.7 1.3 copy-start.10
  48.5 9.9 %copy-start.3 = (bf16[16,112,768]{2,1,0:T(8,128)(2,1)}, bf16[16,112,768]{2,1,0:T(8,128)(2,1)S(1)}, u32[]{:S(2)}) copy-start(bf16[16,112,768]{2,1,0:T(8,128)(2,1)S(1)} %get-tuple-element.43.c_ref) | copy-start | bytes 8257540
  48.5 9.9 %copy-start.6 = (bf16[768,1792]{1,0:T(8,128)(2,1)}, bf16[768,1792]{1,0:T(8,128)(2,1)S(1)}, u32[]{:S(2)}) copy-start(bf16[768,1792]{1,0:T(8,128)(2,1)S(1)} %get-tuple-element.50.c_both.c_ref) | copy-start | bytes 8257540
  55.2 3.2 %copy-start.5 = (bf16[768,1792]{1,0:T(8,128)(2,1)S(1)}, bf16[768,1792]{1,0:T(8,128)(2,1)}, u32[]{:S(2)}) copy-start(bf16[768,1792]{1,0:T(8,128)(2,1)} %copy-done.4) | copy-start | bytes 8257540
  58.3 10.3 %copy-start.14 = (bf16[112,1536]{1,0:T(8,128)(2,1)}, bf16[112,1536]{1,0:T(8,128)(2,1)S(1)}, u32[]{:S(2)}) copy-start(bf16[112,1536]{1,0:T(8,128)(2,1)S(1)} %collective-permute-done.12.e_other_ref) | copy-start | bytes 1032196
  68.6 18.0 %collective-permute-start.15 = (bf16[448,1536]{1,0:T(8,128)(2,1)}, bf16[448,1536]{1,0:T(8,128)(2,1)S(1)}, u32[]{:S(2)}, u32[]{:S(2)}) collective-permute-start(bf16[448,1536]{1,0:T(8,128)(2,1)} %get-tuple-element.64), channel_id=1, source_target_pairs={{0,24},{1,97},{2,26},{3,99},{4,28},{5,101},{6,30},{7,103},{8,0},{9... | collective-permute-start | bytes 4128776 | tf_op jit(solution)/shard_map/ppermute | solution.py:30
  68.7 22.8 %collective-permute-start.17 = (bf16[448,1536]{1,0:T(8,128)(2,1)}, bf16[448,1536]{1,0:T(8,128)(2,1)S(1)}, u32[]{:S(2)}, u32[]{:S(2)}) collective-permute-start(bf16[448,1536]{1,0:T(8,128)(2,1)} %get-tuple-element.66), channel_id=1, source_target_pairs={{0,8},{1,33},{2,10},{3,35},{4,12},{5,37},{6,14},{7,39},{8,16},{9,4... | collective-permute-start | bytes 4128776 | tf_op jit(solution)/shard_map/ppermute | solution.py:30
  70.2 13.9 %all-to-all-start = ((bf16[8,96,224]{2,1,0:T(8,128)(2,1)}), bf16[8,96,224]{2,1,0:T(8,128)(2,1)S(1)}, u32[]{:S(2)}, u32[]{:S(2)}) async-start(bf16[8,96,224]{2,1,0:T(8,128)(2,1)} %get-tuple-element.56), calls=%async_computation | async-start | bytes 786432 | tf_op jit(solution)/shard_map/all_to_all | solution.py:38
  85.2 76.2 %collective-permute-start.14 = (bf16[448,1536]{1,0:T(8,128)(2,1)}, bf16[448,1536]{1,0:T(8,128)(2,1)}, u32[]{:S(2)}, u32[]{:S(2)}) collective-permute-start(bf16[448,1536]{1,0:T(8,128)(2,1)} %get-tuple-element.62), channel_id=1, source_target_pairs={{0,24},{1,97},{2,26},{3,99},{4,28},{5,101},{6,30},{7,103},{8,0},{9... | collective-permute-start | bytes 4128776 | tf_op jit(solution)/shard_map/ppermute | solution.py:30
  85.9 75.5 %collective-permute-start.19 = (bf16[448,1536]{1,0:T(8,128)(2,1)}, bf16[448,1536]{1,0:T(8,128)(2,1)}, u32[]{:S(2)}, u32[]{:S(2)}) collective-permute-start(bf16[448,1536]{1,0:T(8,128)(2,1)} %get-tuple-element.67), channel_id=1, source_target_pairs={{0,8},{1,33},{2,10},{3,35},{4,12},{5,37},{6,14},{7,39},{8,16},{9,4... | collective-permute-start | bytes 4128776 | tf_op jit(solution)/shard_map/ppermute | solution.py:30
  86.6 4.9 %copy-start.19 = (bf16[448,1536]{1,0:T(8,128)(2,1)S(1)}, bf16[448,1536]{1,0:T(8,128)(2,1)}, u32[]{:S(2)}) copy-start(bf16[448,1536]{1,0:T(8,128)(2,1)} %get-tuple-element.65) | copy-start | bytes 4128772
  89.5 71.9 %collective-permute-start.16 = (bf16[448,1536]{1,0:T(8,128)(2,1)}, bf16[448,1536]{1,0:T(8,128)(2,1)}, u32[]{:S(2)}, u32[]{:S(2)}) collective-permute-start(bf16[448,1536]{1,0:T(8,128)(2,1)} %add_convert_fusion.1), channel_id=1, source_target_pairs={{0,24},{1,97},{2,26},{3,99},{4,28},{5,101},{6,30},{7,103},{8,0},{9... | collective-permute-start | bytes 4128776 | tf_op jit(solution)/shard_map/ppermute | solution.py:30
  93.0 68.4 %collective-permute-start.18 = (bf16[448,1536]{1,0:T(8,128)(2,1)}, bf16[448,1536]{1,0:T(8,128)(2,1)}, u32[]{:S(2)}, u32[]{:S(2)}) collective-permute-start(bf16[448,1536]{1,0:T(8,128)(2,1)} %add_convert_fusion), channel_id=1, source_target_pairs={{0,8},{1,33},{2,10},{3,35},{4,12},{5,37},{6,14},{7,39},{8,16},{9,4... | collective-permute-start | bytes 4128776 | tf_op jit(solution)/shard_map/ppermute | solution.py:30
  93.0 33.5 %all-to-all-start.1 = ((bf16[16,96,224]{2,1,0:T(8,128)(2,1)}), bf16[16,96,224]{2,1,0:T(8,128)(2,1)S(1)}, u32[]{:S(2)}, u32[]{:S(2)}) async-start(bf16[16,96,224]{2,1,0:T(8,128)(2,1)} %shard_map.113), calls=%async_computation.1 | async-start | bytes 1572864 | tf_op jit(solution)/shard_map/all_to_all | solution.py:38
  105.3 71.0 %collective-permute-start.13 = (bf16[16,112,384]{2,1,0:T(8,128)(2,1)}, bf16[16,112,384]{2,1,0:T(8,128)(2,1)S(1)}, u32[]{:S(2)}, u32[]{:S(2)}) collective-permute-start(bf16[16,112,384]{2,1,0:T(8,128)(2,1)} %get-tuple-element.55), channel_id=1, source_target_pairs={{0,1},{1,0},{2,3},{3,2},{4,5},{5,4},{6,7},{7,6},{8,9},{9,8},{10,11... | collective-permute-start | bytes 4128776 | tf_op jit(solution)/shard_map/ppermute | solution.py:34
  157.8 20.1 %all-to-all-start.4 = ((bf16[16,96,128]{2,1,0:T(8,128)(2,1)}), bf16[16,96,128]{2,1,0:T(8,128)(2,1)S(1)}, u32[]{:S(2)}, u32[]{:S(2)}) async-start(bf16[16,96,128]{2,1,0:T(8,128)(2,1)} %shard_map.117), calls=%async_computation.4 | async-start | bytes 786432 | tf_op jit(solution)/shard_map/all_to_all | solution.py:38
  168.8 18.6 %collective-permute-start.23 = (bf16[112,1536]{1,0:T(8,128)(2,1)}, bf16[112,1536]{1,0:T(8,128)(2,1)}, u32[]{:S(2)}, u32[]{:S(2)}) collective-permute-start(bf16[112,1536]{1,0:T(8,128)(2,1)} %get-tuple-element.74), channel_id=1, source_target_pairs={{0,96},{1,25},{2,98},{3,27},{4,100},{5,29},{6,102},{7,31},{8,104},... | collective-permute-start | bytes 1032200 | tf_op jit(solution)/shard_map/ppermute | solution.py:30
  177.9 17.0 %copy-start.22 = (bf16[112,1536]{1,0:T(8,128)(2,1)S(1)}, bf16[112,1536]{1,0:T(8,128)(2,1)}, u32[]{:S(2)}) copy-start(bf16[112,1536]{1,0:T(8,128)(2,1)} %get-tuple-element.70) | copy-start | bytes 1032196
  178.6 19.7 %copy-start.21 = (bf16[112,1536]{1,0:T(8,128)(2,1)S(1)}, bf16[112,1536]{1,0:T(8,128)(2,1)}, u32[]{:S(2)}) copy-start(bf16[112,1536]{1,0:T(8,128)(2,1)} %get-tuple-element.72) | copy-start | bytes 1032196
  178.6 24.1 %all-to-all-start.5 = ((bf16[8,96,128]{2,1,0:T(8,128)(2,1)}), bf16[8,96,128]{2,1,0:T(8,128)(2,1)S(1)}, u32[]{:S(2)}, u32[]{:S(2)}) async-start(bf16[8,96,128]{2,1,0:T(8,128)(2,1)} %shard_map.118), calls=%async_computation.5 | async-start | bytes 393216 | tf_op jit(solution)/shard_map/all_to_all | solution.py:38
  184.7 14.5 %collective-permute-start.20 = (bf16[112,1536]{1,0:T(8,128)(2,1)}, bf16[112,1536]{1,0:T(8,128)(2,1)S(1)}, u32[]{:S(2)}, u32[]{:S(2)}) collective-permute-start(bf16[112,1536]{1,0:T(8,128)(2,1)} %get-tuple-element.69), channel_id=1, source_target_pairs={{0,96},{1,25},{2,98},{3,27},{4,100},{5,29},{6,102},{7,31},{8,104},... | collective-permute-start | bytes 1032200 | tf_op jit(solution)/shard_map/ppermute | solution.py:30
  187.1 7.8 %collective-permute-start.21 = (bf16[112,1536]{1,0:T(8,128)(2,1)}, bf16[112,1536]{1,0:T(8,128)(2,1)S(1)}, u32[]{:S(2)}, u32[]{:S(2)}) collective-permute-start(bf16[112,1536]{1,0:T(8,128)(2,1)} %get-tuple-element.71), channel_id=1, source_target_pairs={{0,32},{1,9},{2,34},{3,11},{4,36},{5,13},{6,38},{7,15},{8,40},{9,1... | collective-permute-start | bytes 1032200 | tf_op jit(solution)/shard_map/ppermute | solution.py:30
  187.1 11.2 %collective-permute-start.25 = (bf16[112,1536]{1,0:T(8,128)(2,1)}, bf16[112,1536]{1,0:T(8,128)(2,1)S(1)}, u32[]{:S(2)}, u32[]{:S(2)}) collective-permute-start(bf16[112,1536]{1,0:T(8,128)(2,1)} %get-tuple-element.75), channel_id=1, source_target_pairs={{0,32},{1,9},{2,34},{3,11},{4,36},{5,13},{6,38},{7,15},{8,40},{9,1... | collective-permute-start | bytes 1032200 | tf_op jit(solution)/shard_map/ppermute | solution.py:30
  188.5 14.1 %copy-start.20 = (bf16[112,1536]{1,0:T(8,128)(2,1)S(1)}, bf16[112,1536]{1,0:T(8,128)(2,1)}, u32[]{:S(2)}) copy-start(bf16[112,1536]{1,0:T(8,128)(2,1)} %get-tuple-element.68) | copy-start | bytes 1032196
  188.5 9.8 %collective-permute-start.24 = (bf16[112,1536]{1,0:T(8,128)(2,1)S(1)}, bf16[112,1536]{1,0:T(8,128)(2,1)S(1)}, u32[]{:S(2)}, u32[]{:S(2)}) collective-permute-start(bf16[112,1536]{1,0:T(8,128)(2,1)S(1)} %add_convert_fusion.3), channel_id=1, source_target_pairs={{0,96},{1,25},{2,98},{3,27},{4,100},{5,29},{6,102},{7,31},{8,104},... | collective-permute-start | bytes 1032200 | tf_op jit(solution)/shard_map/ppermute | solution.py:30
  195.0 7.6 %collective-permute-start.22 = (bf16[112,1536]{1,0:T(8,128)(2,1)S(1)}, bf16[112,1536]{1,0:T(8,128)(2,1)S(1)}, u32[]{:S(2)}, u32[]{:S(2)}) collective-permute-start(bf16[112,1536]{1,0:T(8,128)(2,1)S(1)} %add_convert_fusion.5), channel_id=1, source_target_pairs={{0,32},{1,9},{2,34},{3,11},{4,36},{5,13},{6,38},{7,15},{8,40},{9,1... | collective-permute-start | bytes 1032200 | tf_op jit(solution)/shard_map/ppermute | solution.py:30
  198.3 4.5 %copy-start.8 = (bf16[1,112,3072]{2,1,0:T(8,128)(2,1)S(1)}, bf16[1,112,3072]{2,1,0:T(8,128)(2,1)}, u32[]{:S(2)}) copy-start(bf16[1,112,3072]{2,1,0:T(8,128)(2,1)} %param.12) | copy-start | bytes 2064388
  198.3 4.5 %copy-start.15 = (f32[3,32,112]{2,1,0:T(8,128)S(1)}, f32[3,32,112]{2,1,0:T(8,128)}, u32[]{:S(2)}) copy-start(f32[3,32,112]{2,1,0:T(8,128)} %get-tuple-element.61.hats_ref) | copy-start | bytes 129028
  198.3 4.5 %copy-start.17 = (f32[3,32,32]{2,1,0:T(8,128)S(1)}, f32[3,32,32]{2,1,0:T(8,128)}, u32[]{:S(2)}) copy-start(f32[3,32,32]{2,1,0:T(8,128)} %copy-done.16) | copy-start | bytes 36868
  199.2 3.6 %collective-permute-start.26 = (bf16[112,1536]{1,0:T(8,128)(2,1)}, bf16[112,1536]{1,0:T(8,128)(2,1)S(1)}, u32[]{:S(2)}, u32[]{:S(2)}) collective-permute-start(bf16[112,1536]{1,0:T(8,128)(2,1)} %add_convert_fusion.2), channel_id=1, source_target_pairs={{0,1},{1,0},{2,3},{3,2},{4,5},{5,4},{6,7},{7,6},{8,9},{9,8},{10,11... | collective-permute-start | bytes 1032200 | tf_op jit(solution)/shard_map/ppermute | solution.py:34
  202.6 2.5 %copy-start.1 = (f32[3,1024,32]{1,2,0:T(8,128)S(1)}, f32[3,1024,32]{1,2,0:T(8,128)}, u32[]{:S(2)}) copy-start(f32[3,1024,32]{1,2,0:T(8,128)} %param.13) | copy-start | bytes 1179652
  (6 other events, 6.2 us)

commit v2 on v1

--- a/solution.py
+++ b/solution.py
@@ -213,11 +213,12 @@
 
 def late_body(
     scale, groups, place_ref, part_all, t_ref, c_ref, low, high, q_ref, t_both, c_both,
-    e_ref, e_other_ref, grads_ref, far_own, far_other, power_ref, total
+    e_ref, e_other_ref, grads_all, far_own, far_other, power_ref, total, grads_out, far_out, sems
 ):
     tok = t_ref.shape[2] // 2
+    here = pl.program_id(0)
     part_ref = tokens_of(part_all, tok)
-    units = grads_ref.shape[-1] // 3
+    units = part_ref.shape[-1] // 3
     gate_up, back = part_ref[:, : 2 * units], part_ref[:, 2 * units :]
     for b, piece in enumerate((low, high)):
         gate_up = gate_up + dot(pair(t_ref, 2, b, tok), piece[:, : 2 * units], 0, 0)
@@ -226,20 +227,33 @@
     activation, slope = gelu_parts(gate_up[:, :units])
     parts = (back * up_pre * slope, back * activation, activation * up_pre)
     parts = [part.astype(BF) for part in parts]
-    for m, part in enumerate(parts):
-        grads_ref[:, m * units : (m + 1) * units] = part
-    far = weight_part(line(t_ref, 2, tok), line(c_ref, 2, tok), grads_ref).astype(BF)
+    grads = jnp.concatenate(parts, axis=1)
+    grads_out[here] = grads
+    far_out[here] = weight_part(line(t_ref, 2, tok), line(c_ref, 2, tok), grads).astype(BF)
+
+    def copies(k):
+        rows = grads_all.at[pl.ds(k * tok, tok)]
+        return (
+            pltpu.make_async_copy(grads_out.at[k], rows, sems.at[2 * k]),
+            pltpu.make_async_copy(far_out.at[k], (far_own, far_other)[k], sems.at[2 * k + 1]),
+        )
+
+    for k in range(2):
+
+        def leave(k=k):
+            for copy in copies(k):
+                copy.start()
+
+        pl.when(here == k)(leave)
     first = jnp.concatenate([dot(q_ref[m], parts[m], 1, 1) for m in range(2)], axis=0).astype(BF)
     second = dot(q_ref[2], parts[2], 1, 1).astype(BF)
     split = first.shape[0]
     top, bottom = dot(first, tokens_of(t_both, tok)[...]), dot(second, tokens_of(c_both, tok)[...])
 
     def start():
-        far_own[...] = far
         total[:split], total[split:] = top, bottom
 
     def finish():
-        far_other[...] = far
         value = jnp.concatenate([top + total[:split], bottom + total[split:]], axis=0)
         width, rows = value.shape[1], e_ref.shape[0]
         error = e_ref[...].astype(F32) + e_other_ref[...].astype(F32)
@@ -255,6 +269,8 @@
         step = width // groups
         for i in range(groups):
             power_ref[i] = value[:, i * step : (i + 1) * step].astype(BF)
+        for copy in (*copies(0), *copies(1)):
+            copy.wait()
 
     pl.when(pl.program_id(0) == 0)(start)
     pl.when(pl.program_id(0) == 1)(finish)
@@ -463,8 +479,13 @@
         (far_struct((2 * tok, wide)), far_struct(long), far_struct(long), far_struct(mine)),
         grid=(2,),
         ins=[SCALAR] + [WHOLE] * 10,
-        outs=(block, fixed(*long), fixed(*long), fixed(*mine)),
-        scratch=[pltpu.VMEM((3 * rank, width), F32)],
+        outs=(pl.BlockSpec(memory_space=pltpu.HBM),) * 3 + (fixed(*mine),),
+        scratch=[
+            pltpu.VMEM((3 * rank, width), F32),
+            pltpu.VMEM((2, tok, wide), BF),
+            pltpu.VMEM((2, *long), BF),
+            pltpu.SemaphoreType.DMA((4,)),
+        ],
         flops=2 * 2 * tok * 8 * rows * wide,
         vmem=16,
     )(

time: 206 us -> 206 us (level)
  no operation moved by 1% of the time
where the time goes in v2:
time: 206 us; the launch traced here: 204 us
  Pallas kernels  68.4 us (33%)
  starting transfers between devices  54.1 us (26%)
  waiting for transfers between devices  41.2 us (20%)
  blocking collectives  23.7 us (12%)
  local copies, waits for them, and re-layouts  9.33 us (5%)
  other arithmetic  6.77 us (3%)
    ppermute x22, starting transfers between devices, neighbour(): return lax.ppermute(value, NODE_GRP, pairs)  26.9 us
    all_to_all x2, blocking collectives, exchange(): return lax.all_to_all(tiles, axis, split_axis=0, concat_axis=0, tiled=True)  23.7 us
    ppermute x22, waiting for transfers between devices, neighbour(): return lax.ppermute(value, NODE_GRP, pairs)  22.6 us
    all_to_all x4, starting transfers between devices, exchange(): return lax.all_to_all(tiles, axis, split_axis=0, concat_axis=0, tiled=True)  19.7 us
    all_to_all x4, waiting for transfers between devices, exchange(): return lax.all_to_all(tiles, axis, split_axis=0, concat_axis=0, tiled=True)  18.6 us
    pallas_call x2, Pallas kernels, ahead(): call(functools.partial(ahead_body, slots), near_struct((both, wide), F32)...  9.73 us
    pallas_call x1, Pallas kernels, on_device(): call(functools.partial(late_body, grad_scale, groups), (far_struct((2 * t...  9.27 us
    unnamed x46, local copies, waits for them, and re-layouts  9.15 us
  transfers between devices with their start and end apart: 31, of which 8 were waited for; matrix products, arithmetic and copies ran while one was open for 3% of the time, Pallas kernels for 28%

profile of v2, /device:TPU:1, one launch (start us, length us, event | category | flops | bytes accessed | tf_op | source)
XLA Modules:
  0.0 204.5 jit_solution(263338170878355538)
XLA Ops:
  0.6 1.5 collective-permute-start.2
  2.5 1.2 shard_map.102.own_ref
  3.7 2.9 %collective-permute-start.1 = (bf16[112,1536]{1,0:T(8,128)(2,1)S(1)}, bf16[112,1536]{1,0:T(8,128)(2,1)S(1)}, u32[]{:S(2)}, u32[]{:S(2)}) collective-permute-start(bf16[112,1536]{1,0:T(8,128)(2,1)S(1)} %shard_map.102.own_ref), channel_id=1, source_target_pairs={{0,24},{1,97},{2,26},{3,99},{4,28},{5,101},{6,30},{7,103},{8,0},{9... | collective-permute-start | bytes 1032200 | tf_op jit(solution)/shard_map/ppermute | solution.py:30
  7.7 1.3 copy-done.9
  9.1 1.3 copy-done.12
  10.4 1.7 shard_map.103
  12.1 1.6 copy-done.4
  14.2 1.2 shard_map.105
  15.4 2.0 collective-permute-start.5
  17.4 1.1 collective-permute-start.8
  18.5 4.8 %collective-permute-done.4.far_low_ref = bf16[48,1536]{1,0:T(8,128)(2,1)S(1)} collective-permute-done((bf16[48,1536]{1,0:T(8,128)(2,1)S(1)}, bf16[48,1536]{1,0:T(8,128)(2,1)S(1)}, u32[]{:S(2)}, u32[]{:S(2)}) %collective-permute-start.4) | collective-permute-done | bytes 147488 | tf_op jit(solution)/shard_map/ppermute | solution.py:30
  24.2 3.1 %collective-permute-start.7 = (bf16[224,1536]{1,0:T(8,128)(2,1)}, bf16[224,1536]{1,0:T(8,128)(2,1)}, u32[]{:S(2)}, u32[]{:S(2)}) collective-permute-start(bf16[224,1536]{1,0:T(8,128)(2,1)} %shard_map.106.refs_1_), channel_id=1, source_target_pairs={{0,96},{1,25},{2,98},{3,27},{4,100},{5,29},{6,102},{7,31},{8,104},... | collective-permute-start | bytes 2064392 | tf_op jit(solution)/shard_map/ppermute | solution.py:30
  28.8 1.8 collective-permute-done.8.refs_2_.refs_6_
  30.6 4.9 %collective-permute-done.7.refs_1_.refs_3_ = bf16[224,1536]{1,0:T(8,128)(2,1)} collective-permute-done((bf16[224,1536]{1,0:T(8,128)(2,1)}, bf16[224,1536]{1,0:T(8,128)(2,1)}, u32[]{:S(2)}, u32[]{:S(2)}) %collective-permute-start.7) | collective-permute-done | bytes 688160 | tf_op jit(solution)/shard_map/ppermute | solution.py:30
  35.5 3.4 %collective-permute-start.11 = (bf16[224,1536]{1,0:T(8,128)(2,1)}, bf16[224,1536]{1,0:T(8,128)(2,1)}, u32[]{:S(2)}, u32[]{:S(2)}) collective-permute-start(bf16[224,1536]{1,0:T(8,128)(2,1)} %collective-permute-done.7.refs_1_.refs_3_), channel_id=1, source_target_pairs={{0,96},{1,25},{2,98},{3,27},{4,100},{5,29},{6,102},{7,31},{8,104},... | collective-permute-start | bytes 2064392 | tf_op jit(solution)/shard_map/ppermute | solution.py:30
  38.9 1.1 copy-done.7
  41.3 3.3 %collective-permute-start.12 = (bf16[112,1536]{1,0:T(8,128)(2,1)}, bf16[112,1536]{1,0:T(8,128)(2,1)S(1)}, u32[]{:S(2)}, u32[]{:S(2)}) collective-permute-start(bf16[112,1536]{1,0:T(8,128)(2,1)} %copy-done.18), channel_id=1, source_target_pairs={{0,1},{1,0},{2,3},{3,2},{4,5},{5,4},{6,7},{7,6},{8,9},{9,8},{10,11... | collective-permute-start | bytes 1032200 | tf_op jit(solution)/shard_map/ppermute | solution.py:34
  44.7 1.3 copy-done.10
  46.0 2.5 %shard_map.104 = (bf16[16,112,768]{2,1,0:T(8,128)(2,1)S(1)}, bf16[768,1792]{1,0:T(8,128)(2,1)S(1)}) custom-call(s32[18]{0:T(128)S(1)} %pad_add_fusion.place_ref.order_ref.core_ref, bf16[384,1792]{1,0:T(8,128)(2,1)S(1)} %copy-done.10, bf16[384,1792]{1,0:T(8,128)(2,1)} %collective-permute-done.3.other_ref), custom_call_target="tpu_custom_call" | custom-call | tf_op jit(solution)/shard_map/pallas_call | solution.py:151
  48.6 6.6 %shard_map.107.refs_2_ = f32[768,1536]{1,0:T(8,128)S(1)} custom-call(bf16[16,112,768]{2,1,0:T(8,128)(2,1)S(1)} %get-tuple-element.42.t_ref, bf16[16,112,768]{2,1,0:T(8,128)(2,1)S(1)} %get-tuple-element.43.c_ref, bf16[224,1536]{1,0:T(8,128)(2,1)} %get-tuple-element.48.refs_0_, bf16[224,1536]{1,0:T(8,128)(2,1)} %shard_map.106.refs_1_, ...), custom_call_target="tpu_custom_call" | custom-call | flops 2113929216 | bytes 1048576 | tf_op jit(solution)/shard_map/pallas_call | solution.py:198
  55.2 3.1 %shard_map.108.part_all = f32[768,1536]{1,0:T(8,128)S(1)} custom-call(bf16[16,112,768]{2,1,0:T(8,128)(2,1)S(1)} %get-tuple-element.42.t_ref, bf16[16,112,768]{2,1,0:T(8,128)(2,1)S(1)} %get-tuple-element.43.c_ref, bf16[224,1536]{1,0:T(8,128)(2,1)} %collective-permute-done.6.refs_0_.refs_7_, bf16[224,1536]{1,0:T(8,128)(2,1)} %collective-permute-done.7.refs_1_.refs_3_, ...), custom_call_target="tpu_custom_call" | custom-call | flops 1056964608 | bytes 1048576 | tf_op jit(solution)/shard_map/pallas_call | solution.py:198
  58.4 9.3 %shard_map.110 = (bf16[768,1536]{1,0:T(8,128)(2,1)}, bf16[448,1536]{1,0:T(8,128)(2,1)}, bf16[448,1536]{1,0:T(8,128)(2,1)}, bf16[8,96,224]{2,1,0:T(8,128)(2,1)}) custom-call(s32[18]{0:T(128)S(1)} %pad_add_fusion.place_ref.order_ref.core_ref, f32[768,1536]{1,0:T(8,128)S(1)} %shard_map.108.part_all, bf16[16,112,768]{2,1,0:T(8,128)(2,1)S(1)} %get-tuple-element.42.t_ref, ...), custom_call_target="tpu_custom_call" | custom-call | flops 2113929216 | bytes 1048576 | tf_op jit(solution)/shard_map/pallas_call | solution.py:477
  68.0 1.5 collective-permute-start.17
  69.4 6.0 %all-to-all-start = ((bf16[8,96,224]{2,1,0:T(8,128)(2,1)}), bf16[8,96,224]{2,1,0:T(8,128)(2,1)S(1)}, u32[]{:S(2)}, u32[]{:S(2)}) async-start(bf16[8,96,224]{2,1,0:T(8,128)(2,1)} %get-tuple-element.56), calls=%async_computation | async-start | bytes 786432 | tf_op jit(solution)/shard_map/all_to_all | solution.py:38
  75.4 8.0 %shard_map.114 = (bf16[448,1536]{1,0:T(8,128)(2,1)}, bf16[448,1536]{1,0:T(8,128)(2,1)}, bf16[448,1536]{1,0:T(8,128)(2,1)}, bf16[448,1536]{1,0:T(8,128)(2,1)}) custom-call(bf16[4,4,112,768]{3,2,1,0:T(8,128)(2,1)} %bitcast.11, bf16[4,4,112,768]{3,2,1,0:T(8,128)(2,1)} %bitcast.14, bf16[4,4,112,768]{3,2,1,0:T(8,128)(2,1)} %bitcast.12, ...), custom_call_target="tpu_custom_call" | custom-call | flops 2113929216 | bytes 1048576 | tf_op jit(solution)/shard_map/pallas_call | solution.py:498
  85.9 2.9 %add_convert_fusion.1 = bf16[448,1536]{1,0:T(8,128)(2,1)} fusion(bf16[448,1536]{1,0:T(8,128)(2,1)S(1)} %collective-permute-done.15, bf16[448,1536]{1,0:T(8,128)(2,1)} %get-tuple-element.63), kind=kLoop, calls=%fused_computation.1 | loop fusion | flops 2752512 | bytes 4128768 | tf_op jit(solution)/shard_map/convert_element_type | solution.py:517
  88.8 2.0 collective-permute-start.16
  90.8 1.5 add_convert_fusion
  92.2 4.1 %all-to-all-start.1 = ((bf16[16,96,224]{2,1,0:T(8,128)(2,1)}), bf16[16,96,224]{2,1,0:T(8,128)(2,1)S(1)}, u32[]{:S(2)}, u32[]{:S(2)}) async-start(bf16[16,96,224]{2,1,0:T(8,128)(2,1)} %shard_map.113), calls=%async_computation.1 | async-start | bytes 1572864 | tf_op jit(solution)/shard_map/all_to_all | solution.py:38
  96.3 8.2 %shard_map.111 = (bf16[16,112,384]{2,1,0:T(8,128)(2,1)S(1)}, bf16[16,112,384]{2,1,0:T(8,128)(2,1)}) custom-call(s32[18]{0:T(128)S(1)} %pad_add_fusion.place_ref.order_ref.core_ref, bf16[768,1536]{1,0:T(8,128)(2,1)} %get-tuple-element.53.y_ref.grads_ref, bf16[224,1536]{1,0:T(8,128)(2,1)} %get-tuple-element.48.refs_0_, bf16[224,1536]{1,0:T(8,128)(2,1)} %shard_map.106.refs_1_, ...), custom_call_target="tpu_custom_call" | custom-call | flops 2818572288 | bytes 1048576 | tf_op jit(solution)/shard_map/pallas_call | solution.py:563
  104.5 2.6 %collective-permute-start.13 = (bf16[16,112,384]{2,1,0:T(8,128)(2,1)}, bf16[16,112,384]{2,1,0:T(8,128)(2,1)S(1)}, u32[]{:S(2)}, u32[]{:S(2)}) collective-permute-start(bf16[16,112,384]{2,1,0:T(8,128)(2,1)} %get-tuple-element.55), channel_id=1, source_target_pairs={{0,1},{1,0},{2,3},{3,2},{4,5},{5,4},{6,7},{7,6},{8,9},{9,8},{10,11... | collective-permute-start | bytes 4128776 | tf_op jit(solution)/shard_map/ppermute | solution.py:34
  107.2 18.6 %all-to-all-done.1.in_ref = bf16[16,96,224]{2,1,0:T(8,128)(2,1)S(1)} async-done(((bf16[16,96,224]{2,1,0:T(8,128)(2,1)}), bf16[16,96,224]{2,1,0:T(8,128)(2,1)S(1)}, u32[]{:S(2)}, u32[]{:S(2)}) %all-to-all-start.1) | async-done | bytes 688160 | tf_op jit(solution)/shard_map/all_to_all | solution.py:38
  126.6 15.7 %all_to_all.30.p_ref = bf16[8,96,224]{2,1,0:T(8,128)(2,1)S(1)} all-to-all(bf16[8,96,224]{2,1,0:T(8,128)(2,1)} %shard_map.115), channel_id=1, replica_groups=mesh['node_0'=4,'node_1'=4,'grp_0'=4,'grp_1'=2] {'grp_0','grp_1'}, dimensions={0} | all-to-all | bytes 688128 | tf_op jit(solution)/shard_map/all_to_all | solution.py:38
  142.3 6.1 %shard_map.116 = bf16[4,96,128]{2,1,0:T(8,128)(2,1)} custom-call(s32[18]{0:T(128)S(1)} %pad_add_fusion.place_ref.order_ref.core_ref, bf16[8,96,224]{2,1,0:T(8,128)(2,1)S(1)} %all_to_all.30.p_ref, bf16[768,1792]{1,0:T(8,128)(2,1)} %copy-done.4, bf16[768,1792]{1,0:T(8,128)(2,1)} %copy-done.6, bf16[768,1536]{1,0:T(8,128)(2,1)} %get-tuple-element.53.y_ref.grads_ref, ...), custom_call_target="tpu_custom_call" | custom-call | flops 528482304 | bytes 1048576 | tf_op jit(solution)/shard_map/pallas_call | solution.py:541
  148.4 7.9 %all_to_all.31.in_ref = bf16[4,96,128]{2,1,0:T(8,128)(2,1)S(1)} all-to-all(bf16[4,96,128]{2,1,0:T(8,128)(2,1)} %shard_map.116), channel_id=1, replica_groups=mesh['node_0'=4,'node_1'=4,'grp_0'=4,'grp_1'=2] {'grp_0'}, dimensions={0} | all-to-all | bytes 196608 | tf_op jit(solution)/shard_map/all_to_all | solution.py:38
  157.1 3.6 %all-to-all-start.4 = ((bf16[16,96,128]{2,1,0:T(8,128)(2,1)}), bf16[16,96,128]{2,1,0:T(8,128)(2,1)S(1)}, u32[]{:S(2)}, u32[]{:S(2)}) async-start(bf16[16,96,128]{2,1,0:T(8,128)(2,1)} %shard_map.117), calls=%async_computation.4 | async-start | bytes 786432 | tf_op jit(solution)/shard_map/all_to_all | solution.py:38
  160.7 7.3 %shard_map.120 = (bf16[112,1536]{1,0:T(8,128)(2,1)}, bf16[112,1536]{1,0:T(8,128)(2,1)}, bf16[112,1536]{1,0:T(8,128)(2,1)}, bf16[112,1536]{1,0:T(8,128)(2,1)}, bf...) custom-call(bf16[4,4,112,768]{3,2,1,0:T(8,128)(2,1)} %bitcast.13, ...), custom_call_target="tpu_custom_call" | custom-call | flops 1056964608 | bytes 1048576 | tf_op jit(solution)/shard_map/pallas_call | solution.py:521
  168.0 2.6 %collective-permute-start.23 = (bf16[112,1536]{1,0:T(8,128)(2,1)}, bf16[112,1536]{1,0:T(8,128)(2,1)}, u32[]{:S(2)}, u32[]{:S(2)}) collective-permute-start(bf16[112,1536]{1,0:T(8,128)(2,1)} %get-tuple-element.74), channel_id=1, source_target_pairs={{0,96},{1,25},{2,98},{3,27},{4,100},{5,29},{6,102},{7,31},{8,104},... | collective-permute-start | bytes 1032200 | tf_op jit(solution)/shard_map/ppermute | solution.py:30
  170.6 4.5 %shard_map.119 = (f32[3,32,32]{2,1,0:T(8,128)S(1)}, f32[3,32,112]{2,1,0:T(8,128)}) custom-call(s32[18]{0:T(128)S(1)} %pad_add_fusion.place_ref.order_ref.core_ref, bf16[8,96,224]{2,1,0:T(8,128)(2,1)S(1)} %all_to_all.30.p_ref), custom_call_target="tpu_custom_call" | custom-call | flops 16777216 | bytes 1048576 | tf_op jit(solution)/shard_map/pallas_call | solution.py:554
  175.7 1.6 shard_map.112
  178.0 6.1 %all-to-all-start.5 = ((bf16[8,96,128]{2,1,0:T(8,128)(2,1)}), bf16[8,96,128]{2,1,0:T(8,128)(2,1)S(1)}, u32[]{:S(2)}, u32[]{:S(2)}) async-start(bf16[8,96,128]{2,1,0:T(8,128)(2,1)} %shard_map.118), calls=%async_computation.5 | async-start | bytes 393216 | tf_op jit(solution)/shard_map/all_to_all | solution.py:38
  184.1 2.4 %collective-permute-start.20 = (bf16[112,1536]{1,0:T(8,128)(2,1)}, bf16[112,1536]{1,0:T(8,128)(2,1)S(1)}, u32[]{:S(2)}, u32[]{:S(2)}) collective-permute-start(bf16[112,1536]{1,0:T(8,128)(2,1)} %get-tuple-element.69), channel_id=1, source_target_pairs={{0,96},{1,25},{2,98},{3,27},{4,100},{5,29},{6,102},{7,31},{8,104},... | collective-permute-start | bytes 1032200 | tf_op jit(solution)/shard_map/ppermute | solution.py:30
  186.7 1.2 add_convert_fusion.3
  187.9 2.5 %collective-permute-start.24 = (bf16[112,1536]{1,0:T(8,128)(2,1)S(1)}, bf16[112,1536]{1,0:T(8,128)(2,1)S(1)}, u32[]{:S(2)}, u32[]{:S(2)}) collective-permute-start(bf16[112,1536]{1,0:T(8,128)(2,1)S(1)} %add_convert_fusion.3), channel_id=1, source_target_pairs={{0,96},{1,25},{2,98},{3,27},{4,100},{5,29},{6,102},{7,31},{8,104},... | collective-permute-start | bytes 1032200 | tf_op jit(solution)/shard_map/ppermute | solution.py:30
  190.4 3.9 %collective-permute-done.21 = bf16[112,1536]{1,0:T(8,128)(2,1)S(1)} collective-permute-done((bf16[112,1536]{1,0:T(8,128)(2,1)}, bf16[112,1536]{1,0:T(8,128)(2,1)S(1)}, u32[]{:S(2)}, u32[]{:S(2)}) %collective-permute-start.21) | collective-permute-done | bytes 344096 | tf_op jit(solution)/shard_map/ppermute | solution.py:30
  194.5 3.2 %collective-permute-done.25 = bf16[112,1536]{1,0:T(8,128)(2,1)S(1)} collective-permute-done((bf16[112,1536]{1,0:T(8,128)(2,1)}, bf16[112,1536]{1,0:T(8,128)(2,1)S(1)}, u32[]{:S(2)}, u32[]{:S(2)}) %collective-permute-start.25) | collective-permute-done | bytes 344096 | tf_op jit(solution)/shard_map/ppermute | solution.py:30
  198.6 3.4 %collective-permute-done.22 = bf16[112,1536]{1,0:T(8,128)(2,1)S(1)} collective-permute-done((bf16[112,1536]{1,0:T(8,128)(2,1)S(1)}, bf16[112,1536]{1,0:T(8,128)(2,1)S(1)}, u32[]{:S(2)}, u32[]{:S(2)}) %collective-permute-start.22) | collective-permute-done | bytes 344096 | tf_op jit(solution)/shard_map/ppermute | solution.py:30
  202.2 2.3 %shard_map.121 = (bf16[1,112,3072]{2,1,0:T(8,128)(2,1)}, f32[3,32,1024]{2,1,0:T(8,128)}) custom-call(s32[18]{0:T(128)S(1)} %pad_add_fusion.place_ref.order_ref.core_ref, bf16[8,96,128]{2,1,0:T(8,128)(2,1)S(1)} %all-to-all-done.5.b_ref, f32[3,32,32]{2,1,0:T(8,128)S(1)} %copy-done.17, f32[3,32,112]{2,1,0:T(8,128)S(1)} %copy-done.15, ...), custom_call_target="tpu_custom_call" | custom-call | tf_op jit(solution)/shard_map/pallas_call | solution.py:574
  (96 shorter events, 13.0 us)
Async XLA Ops:
  0.6 44.1 %copy-start = (f32[3,1024,32]{1,2,0:T(8,128)S(1)}, f32[3,1024,32]{1,2,0:T(8,128)}, u32[]{:S(2)}) copy-start(f32[3,1024,32]{1,2,0:T(8,128)} %param.13) | copy-start | bytes 1179652
  0.6 6.0 %collective-permute-start.2 = (bf16[384,1792]{1,0:T(8,128)(2,1)}, bf16[384,1792]{1,0:T(8,128)(2,1)S(1)}, u32[]{:S(2)}, u32[]{:S(2)}) collective-permute-start(bf16[384,1792]{1,0:T(8,128)(2,1)} %own_ref.2), channel_id=1, source_target_pairs={{0,1},{1,0},{2,3},{3,2},{4,5},{5,4},{6,7},{7,6},{8,9},{9,8},{10,11... | collective-permute-start | bytes 4128776 | tf_op jit(solution)/shard_map/ppermute | solution.py:34
  3.7 10.0 %collective-permute-start.1 = (bf16[112,1536]{1,0:T(8,128)(2,1)S(1)}, bf16[112,1536]{1,0:T(8,128)(2,1)S(1)}, u32[]{:S(2)}, u32[]{:S(2)}) collective-permute-start(bf16[112,1536]{1,0:T(8,128)(2,1)S(1)} %shard_map.102.own_ref), channel_id=1, source_target_pairs={{0,24},{1,97},{2,26},{3,99},{4,28},{5,101},{6,30},{7,103},{8,0},{9... | collective-permute-start | bytes 1032200 | tf_op jit(solution)/shard_map/ppermute | solution.py:30
  6.6 7.6 %collective-permute-start = (bf16[112,1536]{1,0:T(8,128)(2,1)S(1)}, bf16[112,1536]{1,0:T(8,128)(2,1)S(1)}, u32[]{:S(2)}, u32[]{:S(2)}) collective-permute-start(bf16[112,1536]{1,0:T(8,128)(2,1)S(1)} %shard_map.102.own_ref), channel_id=1, source_target_pairs={{0,8},{1,33},{2,10},{3,35},{4,12},{5,37},{6,14},{7,39},{8,16},{9,4... | collective-permute-start | bytes 1032200 | tf_op jit(solution)/shard_map/ppermute | solution.py:30
  6.6 34.8 %collective-permute-start.3 = (bf16[384,1792]{1,0:T(8,128)(2,1)}, bf16[384,1792]{1,0:T(8,128)(2,1)}, u32[]{:S(2)}, u32[]{:S(2)}) collective-permute-start(bf16[384,1792]{1,0:T(8,128)(2,1)} %own_ref.3), channel_id=1, source_target_pairs={{0,1},{1,0},{2,3},{3,2},{4,5},{5,4},{6,7},{7,6},{8,9},{9,8},{10,11... | collective-permute-start | bytes 4128776 | tf_op jit(solution)/shard_map/ppermute | solution.py:34
  12.1 1.6 copy-start.4
  13.6 44.7 %copy-start.2 = (bf16[16,112,768]{2,1,0:T(8,128)(2,1)}, bf16[16,112,768]{2,1,0:T(8,128)(2,1)S(1)}, u32[]{:S(2)}) copy-start(bf16[16,112,768]{2,1,0:T(8,128)(2,1)S(1)} %get-tuple-element.42.t_ref) | copy-start | bytes 8257540
  15.4 7.9 %collective-permute-start.5 = (bf16[64,1536]{1,0:T(8,128)(2,1)S(1)}, bf16[64,1536]{1,0:T(8,128)(2,1)S(1)}, u32[]{:S(2)}, u32[]{:S(2)}) collective-permute-start(bf16[64,1536]{1,0:T(8,128)(2,1)S(1)} %get-tuple-element.47), channel_id=1, source_target_pairs={{0,24},{1,97},{2,26},{3,99},{4,28},{5,101},{6,30},{7,103},{8,0},{9... | collective-permute-start | bytes 589832 | tf_op jit(solution)/shard_map/ppermute | solution.py:30
  17.4 5.9 %collective-permute-start.4 = (bf16[48,1536]{1,0:T(8,128)(2,1)S(1)}, bf16[48,1536]{1,0:T(8,128)(2,1)S(1)}, u32[]{:S(2)}, u32[]{:S(2)}) collective-permute-start(bf16[48,1536]{1,0:T(8,128)(2,1)S(1)} %get-tuple-element.46), channel_id=1, source_target_pairs={{0,8},{1,33},{2,10},{3,35},{4,12},{5,37},{6,14},{7,39},{8,16},{9,4... | collective-permute-start | bytes 442376 | tf_op jit(solution)/shard_map/ppermute | solution.py:30
  17.4 13.2 %collective-permute-start.8 = (bf16[224,1536]{1,0:T(8,128)(2,1)}, bf16[224,1536]{1,0:T(8,128)(2,1)}, u32[]{:S(2)}, u32[]{:S(2)}) collective-permute-start(bf16[224,1536]{1,0:T(8,128)(2,1)} %get-tuple-element.48.refs_0_), channel_id=1, source_target_pairs={{0,32},{1,9},{2,34},{3,11},{4,36},{5,13},{6,38},{7,15},{8,40},{9,1... | collective-permute-start | bytes 2064392 | tf_op jit(solution)/shard_map/ppermute | solution.py:30
  24.2 11.3 %collective-permute-start.7 = (bf16[224,1536]{1,0:T(8,128)(2,1)}, bf16[224,1536]{1,0:T(8,128)(2,1)}, u32[]{:S(2)}, u32[]{:S(2)}) collective-permute-start(bf16[224,1536]{1,0:T(8,128)(2,1)} %shard_map.106.refs_1_), channel_id=1, source_target_pairs={{0,96},{1,25},{2,98},{3,27},{4,100},{5,29},{6,102},{7,31},{8,104},... | collective-permute-start | bytes 2064392 | tf_op jit(solution)/shard_map/ppermute | solution.py:30
  27.3 21.3 %collective-permute-start.9 = (bf16[224,1536]{1,0:T(8,128)(2,1)}, bf16[224,1536]{1,0:T(8,128)(2,1)}, u32[]{:S(2)}, u32[]{:S(2)}) collective-permute-start(bf16[224,1536]{1,0:T(8,128)(2,1)} %get-tuple-element.48.refs_0_), channel_id=1, source_target_pairs={{0,96},{1,25},{2,98},{3,27},{4,100},{5,29},{6,102},{7,31},{8,104},... | collective-permute-start | bytes 2064392 | tf_op jit(solution)/shard_map/ppermute | solution.py:30
  27.9 27.3 %collective-permute-start.6 = (bf16[224,1536]{1,0:T(8,128)(2,1)}, bf16[224,1536]{1,0:T(8,128)(2,1)}, u32[]{:S(2)}, u32[]{:S(2)}) collective-permute-start(bf16[224,1536]{1,0:T(8,128)(2,1)} %shard_map.106.refs_1_), channel_id=1, source_target_pairs={{0,32},{1,9},{2,34},{3,11},{4,36},{5,13},{6,38},{7,15},{8,40},{9,1... | collective-permute-start | bytes 2064392 | tf_op jit(solution)/shard_map/ppermute | solution.py:30
  30.6 27.7 %collective-permute-start.10 = (bf16[224,1536]{1,0:T(8,128)(2,1)}, bf16[224,1536]{1,0:T(8,128)(2,1)}, u32[]{:S(2)}, u32[]{:S(2)}) collective-permute-start(bf16[224,1536]{1,0:T(8,128)(2,1)} %collective-permute-done.8.refs_2_.refs_6_), channel_id=1, source_target_pairs={{0,32},{1,9},{2,34},{3,11},{4,36},{5,13},{6,38},{7,15},{8,40},{9,1... | collective-permute-start | bytes 2064392 | tf_op jit(solution)/shard_map/ppermute | solution.py:30
  35.5 22.9 %collective-permute-start.11 = (bf16[224,1536]{1,0:T(8,128)(2,1)}, bf16[224,1536]{1,0:T(8,128)(2,1)}, u32[]{:S(2)}, u32[]{:S(2)}) collective-permute-start(bf16[224,1536]{1,0:T(8,128)(2,1)} %collective-permute-done.7.refs_1_.refs_3_), channel_id=1, source_target_pairs={{0,96},{1,25},{2,98},{3,27},{4,100},{5,29},{6,102},{7,31},{8,104},... | collective-permute-start | bytes 2064392 | tf_op jit(solution)/shard_map/ppermute | solution.py:30
  41.3 17.0 %copy-start.13 = (bf16[112,1536]{1,0:T(8,128)(2,1)}, bf16[112,1536]{1,0:T(8,128)(2,1)S(1)}, u32[]{:S(2)}) copy-start(bf16[112,1536]{1,0:T(8,128)(2,1)S(1)} %get-tuple-element.51.e_ref) | copy-start | bytes 1032196
  41.3 17.0 %collective-permute-start.12 = (bf16[112,1536]{1,0:T(8,128)(2,1)}, bf16[112,1536]{1,0:T(8,128)(2,1)S(1)}, u32[]{:S(2)}, u32[]{:S(2)}) collective-permute-start(bf16[112,1536]{1,0:T(8,128)(2,1)} %copy-done.18), channel_id=1, source_target_pairs={{0,1},{1,0},{2,3},{3,2},{4,5},{5,4},{6,7},{7,6},{8,9},{9,8},{10,11... | collective-permute-start | bytes 1032200 | tf_op jit(solution)/shard_map/ppermute | solution.py:34
  44.7 1.3 copy-start.10
  48.5 9.9 %copy-start.3 = (bf16[16,112,768]{2,1,0:T(8,128)(2,1)}, bf16[16,112,768]{2,1,0:T(8,128)(2,1)S(1)}, u32[]{:S(2)}) copy-start(bf16[16,112,768]{2,1,0:T(8,128)(2,1)S(1)} %get-tuple-element.43.c_ref) | copy-start | bytes 8257540
  48.5 9.9 %copy-start.6 = (bf16[768,1792]{1,0:T(8,128)(2,1)}, bf16[768,1792]{1,0:T(8,128)(2,1)S(1)}, u32[]{:S(2)}) copy-start(bf16[768,1792]{1,0:T(8,128)(2,1)S(1)} %get-tuple-element.50.c_both.c_ref) | copy-start | bytes 8257540
  55.2 3.2 %copy-start.5 = (bf16[768,1792]{1,0:T(8,128)(2,1)S(1)}, bf16[768,1792]{1,0:T(8,128)(2,1)}, u32[]{:S(2)}) copy-start(bf16[768,1792]{1,0:T(8,128)(2,1)} %copy-done.4) | copy-start | bytes 8257540
  58.3 9.4 %copy-start.14 = (bf16[112,1536]{1,0:T(8,128)(2,1)}, bf16[112,1536]{1,0:T(8,128)(2,1)S(1)}, u32[]{:S(2)}) copy-start(bf16[112,1536]{1,0:T(8,128)(2,1)S(1)} %collective-permute-done.12.e_other_ref) | copy-start | bytes 1032196
  67.7 18.2 %collective-permute-start.15 = (bf16[448,1536]{1,0:T(8,128)(2,1)}, bf16[448,1536]{1,0:T(8,128)(2,1)S(1)}, u32[]{:S(2)}, u32[]{:S(2)}) collective-permute-start(bf16[448,1536]{1,0:T(8,128)(2,1)} %get-tuple-element.64), channel_id=1, source_target_pairs={{0,24},{1,97},{2,26},{3,99},{4,28},{5,101},{6,30},{7,103},{8,0},{9... | collective-permute-start | bytes 4128776 | tf_op jit(solution)/shard_map/ppermute | solution.py:30
  68.0 22.8 %collective-permute-start.17 = (bf16[448,1536]{1,0:T(8,128)(2,1)}, bf16[448,1536]{1,0:T(8,128)(2,1)S(1)}, u32[]{:S(2)}, u32[]{:S(2)}) collective-permute-start(bf16[448,1536]{1,0:T(8,128)(2,1)} %get-tuple-element.66), channel_id=1, source_target_pairs={{0,8},{1,33},{2,10},{3,35},{4,12},{5,37},{6,14},{7,39},{8,16},{9,4... | collective-permute-start | bytes 4128776 | tf_op jit(solution)/shard_map/ppermute | solution.py:30
  69.4 14.0 %all-to-all-start = ((bf16[8,96,224]{2,1,0:T(8,128)(2,1)}), bf16[8,96,224]{2,1,0:T(8,128)(2,1)S(1)}, u32[]{:S(2)}, u32[]{:S(2)}) async-start(bf16[8,96,224]{2,1,0:T(8,128)(2,1)} %get-tuple-element.56), calls=%async_computation | async-start | bytes 786432 | tf_op jit(solution)/shard_map/all_to_all | solution.py:38
  84.4 76.2 %collective-permute-start.14 = (bf16[448,1536]{1,0:T(8,128)(2,1)}, bf16[448,1536]{1,0:T(8,128)(2,1)}, u32[]{:S(2)}, u32[]{:S(2)}) collective-permute-start(bf16[448,1536]{1,0:T(8,128)(2,1)} %get-tuple-element.62), channel_id=1, source_target_pairs={{0,24},{1,97},{2,26},{3,99},{4,28},{5,101},{6,30},{7,103},{8,0},{9... | collective-permute-start | bytes 4128776 | tf_op jit(solution)/shard_map/ppermute | solution.py:30
  85.2 75.5 %collective-permute-start.19 = (bf16[448,1536]{1,0:T(8,128)(2,1)}, bf16[448,1536]{1,0:T(8,128)(2,1)}, u32[]{:S(2)}, u32[]{:S(2)}) collective-permute-start(bf16[448,1536]{1,0:T(8,128)(2,1)} %get-tuple-element.67), channel_id=1, source_target_pairs={{0,8},{1,33},{2,10},{3,35},{4,12},{5,37},{6,14},{7,39},{8,16},{9,4... | collective-permute-start | bytes 4128776 | tf_op jit(solution)/shard_map/ppermute | solution.py:30
  85.9 4.9 %copy-start.19 = (bf16[448,1536]{1,0:T(8,128)(2,1)S(1)}, bf16[448,1536]{1,0:T(8,128)(2,1)}, u32[]{:S(2)}) copy-start(bf16[448,1536]{1,0:T(8,128)(2,1)} %get-tuple-element.65) | copy-start | bytes 4128772
  88.8 71.9 %collective-permute-start.16 = (bf16[448,1536]{1,0:T(8,128)(2,1)}, bf16[448,1536]{1,0:T(8,128)(2,1)}, u32[]{:S(2)}, u32[]{:S(2)}) collective-permute-start(bf16[448,1536]{1,0:T(8,128)(2,1)} %add_convert_fusion.1), channel_id=1, source_target_pairs={{0,24},{1,97},{2,26},{3,99},{4,28},{5,101},{6,30},{7,103},{8,0},{9... | collective-permute-start | bytes 4128776 | tf_op jit(solution)/shard_map/ppermute | solution.py:30
  92.2 68.5 %collective-permute-start.18 = (bf16[448,1536]{1,0:T(8,128)(2,1)}, bf16[448,1536]{1,0:T(8,128)(2,1)}, u32[]{:S(2)}, u32[]{:S(2)}) collective-permute-start(bf16[448,1536]{1,0:T(8,128)(2,1)} %add_convert_fusion), channel_id=1, source_target_pairs={{0,8},{1,33},{2,10},{3,35},{4,12},{5,37},{6,14},{7,39},{8,16},{9,4... | collective-permute-start | bytes 4128776 | tf_op jit(solution)/shard_map/ppermute | solution.py:30
  92.2 33.5 %all-to-all-start.1 = ((bf16[16,96,224]{2,1,0:T(8,128)(2,1)}), bf16[16,96,224]{2,1,0:T(8,128)(2,1)S(1)}, u32[]{:S(2)}, u32[]{:S(2)}) async-start(bf16[16,96,224]{2,1,0:T(8,128)(2,1)} %shard_map.113), calls=%async_computation.1 | async-start | bytes 1572864 | tf_op jit(solution)/shard_map/all_to_all | solution.py:38
  104.5 71.1 %collective-permute-start.13 = (bf16[16,112,384]{2,1,0:T(8,128)(2,1)}, bf16[16,112,384]{2,1,0:T(8,128)(2,1)S(1)}, u32[]{:S(2)}, u32[]{:S(2)}) collective-permute-start(bf16[16,112,384]{2,1,0:T(8,128)(2,1)} %get-tuple-element.55), channel_id=1, source_target_pairs={{0,1},{1,0},{2,3},{3,2},{4,5},{5,4},{6,7},{7,6},{8,9},{9,8},{10,11... | collective-permute-start | bytes 4128776 | tf_op jit(solution)/shard_map/ppermute | solution.py:34
  157.1 20.2 %all-to-all-start.4 = ((bf16[16,96,128]{2,1,0:T(8,128)(2,1)}), bf16[16,96,128]{2,1,0:T(8,128)(2,1)S(1)}, u32[]{:S(2)}, u32[]{:S(2)}) async-start(bf16[16,96,128]{2,1,0:T(8,128)(2,1)} %shard_map.117), calls=%async_computation.4 | async-start | bytes 786432 | tf_op jit(solution)/shard_map/all_to_all | solution.py:38
  168.0 18.7 %collective-permute-start.23 = (bf16[112,1536]{1,0:T(8,128)(2,1)}, bf16[112,1536]{1,0:T(8,128)(2,1)}, u32[]{:S(2)}, u32[]{:S(2)}) collective-permute-start(bf16[112,1536]{1,0:T(8,128)(2,1)} %get-tuple-element.74), channel_id=1, source_target_pairs={{0,96},{1,25},{2,98},{3,27},{4,100},{5,29},{6,102},{7,31},{8,104},... | collective-permute-start | bytes 1032200 | tf_op jit(solution)/shard_map/ppermute | solution.py:30
  177.3 17.0 %copy-start.22 = (bf16[112,1536]{1,0:T(8,128)(2,1)S(1)}, bf16[112,1536]{1,0:T(8,128)(2,1)}, u32[]{:S(2)}) copy-start(bf16[112,1536]{1,0:T(8,128)(2,1)} %get-tuple-element.70) | copy-start | bytes 1032196
  178.0 19.7 %copy-start.21 = (bf16[112,1536]{1,0:T(8,128)(2,1)S(1)}, bf16[112,1536]{1,0:T(8,128)(2,1)}, u32[]{:S(2)}) copy-start(bf16[112,1536]{1,0:T(8,128)(2,1)} %get-tuple-element.72) | copy-start | bytes 1032196
  178.0 24.1 %all-to-all-start.5 = ((bf16[8,96,128]{2,1,0:T(8,128)(2,1)}), bf16[8,96,128]{2,1,0:T(8,128)(2,1)S(1)}, u32[]{:S(2)}, u32[]{:S(2)}) async-start(bf16[8,96,128]{2,1,0:T(8,128)(2,1)} %shard_map.118), calls=%async_computation.5 | async-start | bytes 393216 | tf_op jit(solution)/shard_map/all_to_all | solution.py:38
  184.1 14.5 %collective-permute-start.20 = (bf16[112,1536]{1,0:T(8,128)(2,1)}, bf16[112,1536]{1,0:T(8,128)(2,1)S(1)}, u32[]{:S(2)}, u32[]{:S(2)}) collective-permute-start(bf16[112,1536]{1,0:T(8,128)(2,1)} %get-tuple-element.69), channel_id=1, source_target_pairs={{0,96},{1,25},{2,98},{3,27},{4,100},{5,29},{6,102},{7,31},{8,104},... | collective-permute-start | bytes 1032200 | tf_op jit(solution)/shard_map/ppermute | solution.py:30
  186.5 7.8 %collective-permute-start.21 = (bf16[112,1536]{1,0:T(8,128)(2,1)}, bf16[112,1536]{1,0:T(8,128)(2,1)S(1)}, u32[]{:S(2)}, u32[]{:S(2)}) collective-permute-start(bf16[112,1536]{1,0:T(8,128)(2,1)} %get-tuple-element.71), channel_id=1, source_target_pairs={{0,32},{1,9},{2,34},{3,11},{4,36},{5,13},{6,38},{7,15},{8,40},{9,1... | collective-permute-start | bytes 1032200 | tf_op jit(solution)/shard_map/ppermute | solution.py:30
  186.5 11.2 %collective-permute-start.25 = (bf16[112,1536]{1,0:T(8,128)(2,1)}, bf16[112,1536]{1,0:T(8,128)(2,1)S(1)}, u32[]{:S(2)}, u32[]{:S(2)}) collective-permute-start(bf16[112,1536]{1,0:T(8,128)(2,1)} %get-tuple-element.75), channel_id=1, source_target_pairs={{0,32},{1,9},{2,34},{3,11},{4,36},{5,13},{6,38},{7,15},{8,40},{9,1... | collective-permute-start | bytes 1032200 | tf_op jit(solution)/shard_map/ppermute | solution.py:30
  187.9 14.1 %copy-start.20 = (bf16[112,1536]{1,0:T(8,128)(2,1)S(1)}, bf16[112,1536]{1,0:T(8,128)(2,1)}, u32[]{:S(2)}) copy-start(bf16[112,1536]{1,0:T(8,128)(2,1)} %get-tuple-element.68) | copy-start | bytes 1032196
  187.9 9.8 %collective-permute-start.24 = (bf16[112,1536]{1,0:T(8,128)(2,1)S(1)}, bf16[112,1536]{1,0:T(8,128)(2,1)S(1)}, u32[]{:S(2)}, u32[]{:S(2)}) collective-permute-start(bf16[112,1536]{1,0:T(8,128)(2,1)S(1)} %add_convert_fusion.3), channel_id=1, source_target_pairs={{0,96},{1,25},{2,98},{3,27},{4,100},{5,29},{6,102},{7,31},{8,104},... | collective-permute-start | bytes 1032200 | tf_op jit(solution)/shard_map/ppermute | solution.py:30
  194.4 7.6 %collective-permute-start.22 = (bf16[112,1536]{1,0:T(8,128)(2,1)S(1)}, bf16[112,1536]{1,0:T(8,128)(2,1)S(1)}, u32[]{:S(2)}, u32[]{:S(2)}) collective-permute-start(bf16[112,1536]{1,0:T(8,128)(2,1)S(1)} %add_convert_fusion.5), channel_id=1, source_target_pairs={{0,32},{1,9},{2,34},{3,11},{4,36},{5,13},{6,38},{7,15},{8,40},{9,1... | collective-permute-start | bytes 1032200 | tf_op jit(solution)/shard_map/ppermute | solution.py:30
  197.7 4.5 %copy-start.8 = (bf16[1,112,3072]{2,1,0:T(8,128)(2,1)S(1)}, bf16[1,112,3072]{2,1,0:T(8,128)(2,1)}, u32[]{:S(2)}) copy-start(bf16[1,112,3072]{2,1,0:T(8,128)(2,1)} %param.12) | copy-start | bytes 2064388
  197.7 4.5 %copy-start.15 = (f32[3,32,112]{2,1,0:T(8,128)S(1)}, f32[3,32,112]{2,1,0:T(8,128)}, u32[]{:S(2)}) copy-start(f32[3,32,112]{2,1,0:T(8,128)} %get-tuple-element.61.hats_ref) | copy-start | bytes 129028
  197.7 4.5 %copy-start.17 = (f32[3,32,32]{2,1,0:T(8,128)S(1)}, f32[3,32,32]{2,1,0:T(8,128)}, u32[]{:S(2)}) copy-start(f32[3,32,32]{2,1,0:T(8,128)} %copy-done.16) | copy-start | bytes 36868
  198.6 3.6 %collective-permute-start.26 = (bf16[112,1536]{1,0:T(8,128)(2,1)}, bf16[112,1536]{1,0:T(8,128)(2,1)S(1)}, u32[]{:S(2)}, u32[]{:S(2)}) collective-permute-start(bf16[112,1536]{1,0:T(8,128)(2,1)} %add_convert_fusion.2), channel_id=1, source_target_pairs={{0,1},{1,0},{2,3},{3,2},{4,5},{5,4},{6,7},{7,6},{8,9},{9,8},{10,11... | collective-permute-start | bytes 1032200 | tf_op jit(solution)/shard_map/ppermute | solution.py:34
  202.0 2.5 %copy-start.1 = (f32[3,1024,32]{1,2,0:T(8,128)S(1)}, f32[3,1024,32]{1,2,0:T(8,128)}, u32[]{:S(2)}) copy-start(f32[3,1024,32]{1,2,0:T(8,128)} %param.13) | copy-start | bytes 1179652
  (6 other events, 6.2 us)
